TPU v7x, 128 devices: a whole 4x4x4 slice. The times are simulated.
128 devices in a mesh: stage: 1, data: 64 (over z, y, x), tp: 2 (over core).
Axes of the slice: x: 4, y: 4, z: 4, core: 2. Of those that a mesh axis runs over, the one named last changes fastest.
Arguments:
- weight: float32 [12, 576, 1536], P('stage', None, 'tp')
- momentum: float32 [12, 576, 1536], P('stage', None, 'tp')
- grad: bfloat16 [12, 64, 576, 1536], P('stage', 'data', None, 'tp')
Outputs:
- output 1: float32 [12, 576, 1536], P('stage', None, 'tp')
- output 2: float32 [12, 576, 1536], P('stage', None, 'tp')
All inputs are finite; a program needn't handle non-finite values.
Results may differ from a plain program's by a relative error of at most 0.0155555.
Values are sent between devices in bfloat16 or wider.
A program may use at most 1 GiB of HBM per device.

v0:
```python
import math
import jax
import jax.numpy as jnp
from jax import lax
from jax.sharding import PartitionSpec as P

MOMENTUM = 0.95
LEARN_RATE = 0.25
WEIGHT_DECAY = 0.1
COEF_A = 3.4445
COEF_B = -4.7750
COEF_C = 2.0315
NORM_EPS = 1e-7
NS_STEPS = 5


def solution(mesh):
    data_size = mesh.shape["data"]
    tp_size = mesh.shape["tp"]
    state_spec = P("stage", None, "tp")
    grad_spec = P("stage", "data", None, "tp")

    def per_device(weight, momentum, grad):
        row_count = weight.shape[1]
        col_count = weight.shape[2] * tp_size
        grad_sum = jnp.sum(grad, axis=1, dtype=jnp.float32)
        grad_mean = lax.psum(grad_sum, "data") / data_size
        new_mom = MOMENTUM * momentum + grad_mean
        nesterov = grad_mean + MOMENTUM * new_mom
        square_part = jnp.sum(nesterov * nesterov, axis=(1, 2), keepdims=True)
        norms = jnp.sqrt(lax.psum(square_part, "tp"))
        ortho = (nesterov / (norms + NORM_EPS)).astype(jnp.bfloat16)
        for step_idx in range(NS_STEPS):
            part_gram = jnp.einsum("lik,ljk->lij", ortho, ortho, preferred_element_type=jnp.float32)
            gram_mat = lax.psum(part_gram, "tp").astype(jnp.bfloat16)
            square_mat = jnp.einsum("lij,ljk->lik", gram_mat, gram_mat, preferred_element_type=jnp.float32)
            poly_mat = (COEF_B * gram_mat.astype(jnp.float32) + COEF_C * square_mat).astype(jnp.bfloat16)
            update = jnp.einsum("lij,ljk->lik", poly_mat, ortho, preferred_element_type=jnp.float32)
            ortho = (COEF_A * ortho.astype(jnp.float32) + update).astype(jnp.bfloat16)
        rms_scale = 0.2 * math.sqrt(max(row_count, col_count))
        new_weight = weight - LEARN_RATE * (rms_scale * ortho.astype(jnp.float32) + WEIGHT_DECAY * weight)
        return new_weight, new_mom

    return jax.shard_map(per_device, mesh=mesh, in_specs=(state_spec, state_spec, grad_spec), out_specs=(state_spec, state_spec), check_vma=False)
```

profile of v0, /device:TPU:1, one launch (start us, length us, event | category | flops | bytes accessed | tf_op | source)
XLA Modules:
  0.0 803.9 jit_solution(5113545670590981349)
XLA Ops:
  7.2 0.0 all-reduce.7.cloned.1.call-start
  7.2 11.6 %bitcast_convert_fusion = f32[12,576,768]{2,1,0:T(8,128)} fusion(bf16[12,1,576,768]{3,2,1,0:T(8,128)(2,1)} %param.5), kind=kLoop, calls=%fused_computation.15 | loop fusion | flops 5308416 | bytes 31850496 | tf_op jit(solution)/shard_map/reduce_sum | solution.py:26
  18.8 0.0 all-reduce.7.cloned.1.call-update
  18.8 241.8 %all-reduce.7.cloned.1.call-done = f32[12,576,768]{2,1,0:T(8,128)} async-done(((f32[12,576,768]{2,1,0:T(8,128)}), f32[12,576,768]{2,1,0:T(8,128)}) %all-reduce.7.cloned.1.call-update) | async-done | bytes 21233680 | tf_op jit(solution)/shard_map/psum | solution.py:27
  260.6 21.4 %multiply_reduce_fusion = (f32[12]{0:T(128)S(1)}, f32[12,576,768]{2,1,0:T(8,128)}) fusion(f32[12,576,768]{2,1,0:T(8,128)} %all-reduce.7.cloned.1.call-done, f32[12,576,768]{2,1,0:T(8,128)} %param.4), kind=kLoop, calls=%fused_computation.7 | loop fusion | flops 37158900 | bytes 63701040 | tf_op jit(solution)/shard_map/reduce_sum | solution.py:30
  282.0 4.1 psum.50
  286.1 18.2 %divide_convert_fusion = bf16[12,576,768]{2,1,0:T(8,128)(2,1)} fusion(f32[12]{0:T(128)S(1)} %add_bitcast_fusion, f32[12,576,768]{2,1,0:T(8,128)} %get-tuple-element.3, f32[12,576,768]{2,1,0:T(8,128)} %all-reduce.7.cloned.1.call-done), kind=kLoop, calls=%fused_computation.6 | loop fusion | flops 26542080 | bytes 53084208 | tf_op jit(solution)/shard_map/convert_element_type | solution.py:32
  304.4 17.8 %fusion.53 = f32[12,576,576]{2,1,0:T(8,128)} fusion(bf16[12,576,768]{2,1,0:T(8,128)(2,1)} %divide_convert_fusion), kind=kOutput, calls=%fused_computation.52 | convolution fusion | flops 6115295232 | bytes 26542080 | tf_op jit(solution)/shard_map/lik,ljk->lij/dot_general | solution.py:34
  322.2 48.7 %all-reduce.8 = bf16[12,576,576]{2,1,0:T(8,128)(2,1)} all-reduce(f32[12,576,576]{2,1,0:T(8,128)} %fusion.53), channel_id=1, replica_groups=mesh['stage'=1,'data'=64,'tp'=2] {'tp'}, use_global_device_ids=true, to_apply=%region_3.0 | all-reduce | flops 3981312 | bytes 23887872 | tf_op jit(solution)/shard_map/psum | solution.py:35
  370.9 30.7 %add_convert_fusion.4 = bf16[12,576,768]{2,1,0:T(8,128)(2,1)} fusion(bf16[12,576,768]{2,1,0:T(8,128)(2,1)} %divide_convert_fusion, bf16[12,576,576]{2,1,0:T(8,128)(2,1)} %all-reduce.8), kind=kOutput, calls=%fused_computation.5 | convolution fusion | flops 10742906880 | bytes 29196288 | tf_op jit(solution)/shard_map/lij,ljk->lik/dot_general | solution.py:38
  401.6 17.8 %fusion.54 = f32[12,576,576]{2,1,0:T(8,128)} fusion(bf16[12,576,768]{2,1,0:T(8,128)(2,1)} %add_convert_fusion.4), kind=kOutput, calls=%fused_computation.53 | convolution fusion | flops 6115295232 | bytes 26542080 | tf_op jit(solution)/shard_map/lik,ljk->lij/dot_general | solution.py:34
  419.4 48.6 %all-reduce.9 = bf16[12,576,576]{2,1,0:T(8,128)(2,1)} all-reduce(f32[12,576,576]{2,1,0:T(8,128)} %fusion.54), channel_id=1, replica_groups=mesh['stage'=1,'data'=64,'tp'=2] {'tp'}, use_global_device_ids=true, to_apply=%region_4.0 | all-reduce | flops 3981312 | bytes 23887872 | tf_op jit(solution)/shard_map/psum | solution.py:35
  468.0 30.2 %add_convert_fusion.3 = bf16[12,576,768]{2,1,0:T(8,128)(2,1)} fusion(bf16[12,576,768]{2,1,0:T(8,128)(2,1)} %add_convert_fusion.4, bf16[12,576,576]{2,1,0:T(8,128)(2,1)} %all-reduce.9), kind=kOutput, calls=%fused_computation.4 | convolution fusion | flops 10742906880 | bytes 29196288 | tf_op jit(solution)/shard_map/lij,ljk->lik/dot_general | solution.py:38
  498.2 17.8 %fusion.55 = f32[12,576,576]{2,1,0:T(8,128)} fusion(bf16[12,576,768]{2,1,0:T(8,128)(2,1)} %add_convert_fusion.3), kind=kOutput, calls=%fused_computation.54 | convolution fusion | flops 6115295232 | bytes 26542080 | tf_op jit(solution)/shard_map/lik,ljk->lij/dot_general | solution.py:34
  516.0 48.8 %all-reduce.10 = bf16[12,576,576]{2,1,0:T(8,128)(2,1)} all-reduce(f32[12,576,576]{2,1,0:T(8,128)} %fusion.55), channel_id=1, replica_groups=mesh['stage'=1,'data'=64,'tp'=2] {'tp'}, use_global_device_ids=true, to_apply=%region_5.0 | all-reduce | flops 3981312 | bytes 23887872 | tf_op jit(solution)/shard_map/psum | solution.py:35
  564.9 30.7 %add_convert_fusion.2 = bf16[12,576,768]{2,1,0:T(8,128)(2,1)} fusion(bf16[12,576,768]{2,1,0:T(8,128)(2,1)} %add_convert_fusion.3, bf16[12,576,576]{2,1,0:T(8,128)(2,1)} %all-reduce.10), kind=kOutput, calls=%fused_computation.3 | convolution fusion | flops 10742906880 | bytes 29196288 | tf_op jit(solution)/shard_map/lij,ljk->lik/dot_general | solution.py:38
  595.5 17.8 %fusion.56 = f32[12,576,576]{2,1,0:T(8,128)} fusion(bf16[12,576,768]{2,1,0:T(8,128)(2,1)} %add_convert_fusion.2), kind=kOutput, calls=%fused_computation.55 | convolution fusion | flops 6115295232 | bytes 26542080 | tf_op jit(solution)/shard_map/lik,ljk->lij/dot_general | solution.py:34
  613.3 48.6 %all-reduce.11 = bf16[12,576,576]{2,1,0:T(8,128)(2,1)} all-reduce(f32[12,576,576]{2,1,0:T(8,128)} %fusion.56), channel_id=1, replica_groups=mesh['stage'=1,'data'=64,'tp'=2] {'tp'}, use_global_device_ids=true, to_apply=%region_6.0 | all-reduce | flops 3981312 | bytes 23887872 | tf_op jit(solution)/shard_map/psum | solution.py:35
  661.9 30.2 %add_convert_fusion.1 = bf16[12,576,768]{2,1,0:T(8,128)(2,1)} fusion(bf16[12,576,768]{2,1,0:T(8,128)(2,1)} %add_convert_fusion.2, bf16[12,576,576]{2,1,0:T(8,128)(2,1)} %all-reduce.11), kind=kOutput, calls=%fused_computation.2 | convolution fusion | flops 10742906880 | bytes 29196288 | tf_op jit(solution)/shard_map/lij,ljk->lik/dot_general | solution.py:38
  692.1 17.8 %fusion.57 = f32[12,576,576]{2,1,0:T(8,128)} fusion(bf16[12,576,768]{2,1,0:T(8,128)(2,1)} %add_convert_fusion.1), kind=kOutput, calls=%fused_computation.56 | convolution fusion | flops 6115295232 | bytes 26542080 | tf_op jit(solution)/shard_map/lik,ljk->lij/dot_general | solution.py:34
  709.9 48.8 %all-reduce.12 = bf16[12,576,576]{2,1,0:T(8,128)(2,1)} all-reduce(f32[12,576,576]{2,1,0:T(8,128)} %fusion.57), channel_id=1, replica_groups=mesh['stage'=1,'data'=64,'tp'=2] {'tp'}, use_global_device_ids=true, to_apply=%region_7.0 | all-reduce | flops 3981312 | bytes 23887872 | tf_op jit(solution)/shard_map/psum | solution.py:35
  758.7 38.1 %multiply_subtract_fusion = f32[12,576,768]{2,1,0:T(8,128)} fusion(f32[12,576,768]{2,1,0:T(8,128)} %param.3, bf16[12,576,768]{2,1,0:T(8,128)(2,1)} %add_convert_fusion.1, bf16[12,576,576]{2,1,0:T(8,128)(2,1)} %all-reduce.12), kind=kOutput, calls=%fused_computation | convolution fusion | flops 10774757376 | bytes 61046784 | tf_op jit(solution)/shard_map/lij,ljk->lik/dot_general | solution.py:38
  (1 shorter events, 0.0 us)
Async XLA Ops:
  7.2 253.4 %all-reduce.7.cloned.1.call-start = ((), (), s32[]{:S(2)}) async-start(), calls=%async_computation | async-start | bytes 42467328 | tf_op jit(solution)/shard_map/psum | solution.py:27
Sparse Core Ops, SparseCore 0:
  18.9 241.5 all-reduce.6
where the time goes:
time: 809 us; the launch traced here: 804 us
  matrix products  249 us (31%)
  blocking collectives  248 us (31%)
  waiting for transfers between devices  242 us (30%)
  other arithmetic  51.3 us (6%)
  between operations  14.3 us (2%)
    psum x5, blocking collectives, per_device(): gram_mat = lax.psum(part_gram, 'tp').astype(jnp.bfloat16)  244 us
    psum x1, waiting for transfers between devices, per_device(): grad_mean = lax.psum(grad_sum, 'data') / data_size  242 us
    dot_general x5, matrix products, per_device(): jnp.einsum('lij,ljk->lik', poly_mat, ortho, preferred_element_type=jnp.fl...  160 us
    dot_general x5, matrix products, per_device(): jnp.einsum('lik,ljk->lij', ortho, ortho, preferred_element_type=jnp.float32)  89 us
    reduce_sum x1, other arithmetic, per_device(): square_part = jnp.sum(nesterov * nesterov, axis=(1, 2), keepdims=True)  21.4 us
    convert_element_type x1, other arithmetic, per_device(): ortho = (nesterov / (norms + NORM_EPS)).astype(jnp.bfloat16)  18.2 us
  transfers between devices with their start and end apart: 1, of which 1 were waited for; matrix products, arithmetic and copies ran while one was open for 0% of the time, Pallas kernels for 0%

commit v1 on v0

v1 whole, which is shorter than its diff:
```python
import math
import jax
import jax.numpy as jnp
from jax import lax
from jax.sharding import PartitionSpec as P

MOMENTUM = 0.95
LEARN_RATE = 0.25
WEIGHT_DECAY = 0.1
COEF_A = 3.4445
COEF_B = -4.7750
COEF_C = 2.0315
NORM_EPS = 1e-7
NS_STEPS = 5


def to_tiles(arr):
    layers, rows, cols = arr.shape
    arr = arr.reshape(layers, rows // 8, 8, cols // 128, 128).transpose(0, 1, 3, 2, 4)
    return arr.reshape(layers * (rows // 8) * (cols // 128), 8, 128)


def from_tiles(tiles, layers, rows, cols):
    arr = tiles.reshape(layers, rows // 8, cols // 128, 8, 128).transpose(0, 1, 3, 2, 4)
    return arr.reshape(layers, rows, cols)


def dot_nn(lhs, rhs):
    return lax.dot_general(lhs, rhs, (((1,), (0,)), ((), ())), preferred_element_type=jnp.float32)


def dot_nt(lhs, rhs):
    return lax.dot_general(lhs, rhs, (((1,), (1,)), ((), ())), preferred_element_type=jnp.float32)


def solution(mesh):
    data_size = mesh.shape["data"]
    tp_size = mesh.shape["tp"]
    state_spec = P("stage", None, "tp")
    grad_spec = P("stage", "data", None, "tp")
    swap = [(0, 1), (1, 0)]

    def per_device(weight, momentum, grad):
        layers, rows, cols = weight.shape
        tiles_each = (rows // 8) * (cols // 128)
        share = layers * tiles_each // data_size
        data_idx = lax.axis_index("data")
        tp_idx = lax.axis_index("tp")

        grad_tiles = to_tiles(grad[:, 0].astype(jnp.float32))
        own = lax.psum_scatter(grad_tiles, "data", scatter_dimension=0, tiled=True) / data_size
        grad_mean = from_tiles(lax.all_gather(own, "data", axis=0, tiled=True), layers, rows, cols)
        new_mom = MOMENTUM * momentum + grad_mean

        first = (data_idx * share) // tiles_each
        last = (data_idx * share + share - 1) // tiles_each
        mine = jnp.where(tp_idx == 0, first, last)
        other = jnp.where(tp_idx == 0, last, first)

        def nesterov_of(which):
            mean = lax.dynamic_index_in_dim(grad_mean, which, 0, keepdims=False)
            mom = lax.dynamic_index_in_dim(momentum, which, 0, keepdims=False)
            return mean + MOMENTUM * (MOMENTUM * mom + mean)

        here = nesterov_of(mine)
        there = lax.ppermute(nesterov_of(other), "tp", swap)
        is_left = tp_idx == 0
        full = jnp.concatenate([jnp.where(is_left, here, there), jnp.where(is_left, there, here)], axis=1)
        norm = jnp.sqrt(jnp.sum(full * full))
        ortho = (full / (norm + NORM_EPS)).astype(jnp.bfloat16)
        for step_idx in range(NS_STEPS):
            gram_mat = dot_nt(ortho, ortho).astype(jnp.bfloat16)
            square_mat = dot_nn(gram_mat, gram_mat)
            poly_mat = (COEF_B * gram_mat.astype(jnp.float32) + COEF_C * square_mat).astype(jnp.bfloat16)
            update = dot_nn(poly_mat, ortho)
            ortho = (COEF_A * ortho.astype(jnp.float32) + update).astype(jnp.bfloat16)
        left, right = ortho[:, :cols], ortho[:, cols:]
        keep = jnp.where(is_left, left, right)
        got = lax.ppermute(jnp.where(is_left, right, left), "tp", swap)
        pair = jnp.stack([jnp.where(is_left, keep, got), jnp.where(is_left, got, keep)])
        piece = lax.dynamic_slice_in_dim(to_tiles(pair), data_idx * share - first * tiles_each, share, 0)
        ortho_all = from_tiles(lax.all_gather(piece, "data", axis=0, tiled=True), layers, rows, cols)
        rms_scale = 0.2 * math.sqrt(max(rows, cols * tp_size))
        new_weight = weight - LEARN_RATE * (rms_scale * ortho_all.astype(jnp.float32) + WEIGHT_DECAY * weight)
        return new_weight, new_mom

    return jax.shard_map(per_device, mesh=mesh, in_specs=(state_spec, state_spec, grad_spec), out_specs=(state_spec, state_spec), check_vma=False)
```

time: 809 us -> 545 us (0.67)
  blocking collectives: 248 us -> 0 us
  matrix products: 249 us -> 31.7 us
  waiting for transfers between devices: 242 us -> 430 us
  other arithmetic: 51.3 us -> 64.1 us
    psum x6 -> x0, blocking collectives: 248 us -> none  [the longest x5 244 us: per_device(): gram_mat = lax.psum(part_gram, 'tp').astype(jnp.bfloat16)]
    unnamed x1 -> x4, waiting for transfers between devices: 0.02 us -> 244 us
    psum x1 -> x0, waiting for transfers between devices: 242 us -> none  [per_device(): grad_mean = lax.psum(grad_sum, 'data') / data_size]
    dot_general x10, matrix products: 249 us -> 31.7 us  [the longest x5 20.4 us: dot_nn(): lax.dot_general(lhs, rhs, (((1,), (0,)), ((), ())), preferred_element_typ...]
    all_gather x0 -> x2, waiting for transfers between devices: none -> 181 us  [the longest x1 118 us: per_device(): lax.all_gather(own, 'data', axis=0, tiled=True)]
    reduce_sum x2 -> x1, other arithmetic: 33 us -> 1.51 us  [per_device(): norm = jnp.sqrt(jnp.sum(full * full))]
    add x0 -> x2, other arithmetic: none -> 24 us  [the longest x1 21.7 us: per_device(): new_mom = MOMENTUM * momentum + grad_mean]
    convert_element_type x1, other arithmetic: 18.2 us -> 0.25 us  [per_device(): ortho = (full / (norm + NORM_EPS)).astype(jnp.bfloat16)]
  transfers between devices with their start and end apart: 1 -> 5, of which waited for: 1 -> 5; matrix products, arithmetic and copies ran while one was open for 0% -> 4% of each run, Pallas kernels for 0% -> 0%
where the time goes in v1:
time: 545 us; the launch traced here: 544 us
  waiting for transfers between devices  430 us (79%)
  other arithmetic  64.1 us (12%)
  matrix products  31.7 us (6%)
  between operations  14.6 us (3%)
    unnamed x4, waiting for transfers between devices  244 us
    all_gather x1, waiting for transfers between devices, per_device(): lax.all_gather(own, 'data', axis=0, tiled=True)  118 us
    all_gather x1, waiting for transfers between devices, per_device(): lax.all_gather(piece, 'data', axis=0, tiled=True)  62.3 us
    add x1, other arithmetic, per_device(): new_mom = MOMENTUM * momentum + grad_mean  21.7 us
    dot_general x5, matrix products, dot_nn(): lax.dot_general(lhs, rhs, (((1,), (0,)), ((), ())), preferred_element_typ...  20.4 us
    sub x1, other arithmetic, per_device(): weight - LEARN_RATE * (rms_scale * ortho_all.astype(jnp.float32) + WEIGHT...  15.7 us
    reshape x1, other arithmetic, to_tiles(): return arr.reshape(layers * (rows // 8) * (cols // 128), 8, 128)  11.6 us
    dot_general x5, matrix products, dot_nt(): lax.dot_general(lhs, rhs, (((1,), (1,)), ((), ())), preferred_element_typ...  11.3 us
  transfers between devices with their start and end apart: 5, of which 5 were waited for; matrix products, arithmetic and copies ran while one was open for 4% of the time, Pallas kernels for 0%

profile of v1, /device:TPU:1, one launch (start us, length us, event | category | flops | bytes accessed | tf_op | source)
XLA Modules:
  0.0 544.0 jit_solution(16703994525652665143)
XLA Ops:
  7.2 0.0 reduce-scatter.4.cloned.1.call-start
  7.2 11.6 %bitcast_convert_fusion = f32[12,72,8,6,128]{4,2,3,1,0:T(8,128)} fusion(bf16[12,1,576,768]{3,2,1,0:T(8,128)(2,1)} %param.5), kind=kLoop, calls=%fused_computation.5 | loop fusion | flops 5308416 | bytes 31850496 | tf_op jit(solution)/shard_map/reshape | solution.py:20
  18.8 0.0 reduce-scatter.4.cloned.1.call-update
  18.8 0.0 all-gather.3.cloned.1.call-start
  18.9 244.2 %reduce-scatter.4.cloned.1.call-done = f32[81,8,128]{2,1,0:T(8,128)} async-done(((f32[5184,8,128]{2,1,0:T(8,128)}), f32[81,8,128]{2,1,0:T(8,128)}) %reduce-scatter.4.cloned.1.call-update) | async-done | bytes 331792
  263.1 1.7 broadcast_multiply_fusion
  264.8 0.0 all-gather.3.cloned.1.call-update
  264.8 0.0 all-gather.5.cloned.1.call-start
  264.9 118.2 %all-gather.3.cloned.1.call-done = f32[5184,8,128]{2,1,0:T(8,128)} async-done(((f32[81,8,128]{2,1,0:T(8,128)}), f32[5184,8,128]{2,1,0:T(8,128)}) %all-gather.3.cloned.1.call-update) | async-done | bytes 21233680 | tf_op jit(solution)/shard_map/all_gather | solution.py:52
  383.2 2.3 fusion.3
  385.5 1.0 collective-permute-start
  386.5 3.3 collective-permute-done
  389.8 2.9 broadcast_select_fusion.3
  392.7 1.5 multiply_reduce_fusion
  394.9 0.2 divide_convert_fusion
  395.2 0.0 copy-start
  395.2 1.2 copy-done
  396.4 1.6 convolution_convert_fusion.4
  397.9 4.2 add_convert_fusion.4
  402.1 2.4 convolution_convert_fusion.3
  404.6 4.0 add_convert_fusion.3
  408.6 2.4 convolution_convert_fusion.2
  411.0 4.0 add_convert_fusion.2
  415.0 2.4 convolution_convert_fusion.1
  417.4 4.0 add_convert_fusion.1
  421.5 2.4 convolution_convert_fusion
  423.9 4.2 add_convert_fusion
  428.1 0.1 broadcast_select_fusion
  428.2 0.4 collective-permute-start.1
  428.6 2.1 collective-permute-done.1
  430.7 0.2 select_bitcast_fusion.1
  430.9 0.2 pad_maximum_fusion.1
  431.0 0.7 constant_dynamic-slice_fusion
  431.7 0.0 all-gather.5.cloned.1.call-update
  431.7 21.7 %multiply_add_fusion = f32[12,576,768]{2,1,0:T(8,128)} fusion(f32[12,576,768]{2,1,0:T(8,128)} %param.4, f32[12,576,768]{2,1,0:T(8,128)} %bitcast.85), kind=kLoop, calls=%fused_computation.3 | loop fusion | flops 10616832 | bytes 63700992 | tf_op jit(solution)/shard_map/add | solution.py:53
  453.4 62.3 %all-gather.5.cloned.1.call-done = bf16[5184,8,128]{2,1,0:T(8,128)(2,1)} async-done(((bf16[81,8,128]{2,1,0:T(8,128)(2,1)}), bf16[5184,8,128]{2,1,0:T(8,128)(2,1)}) %all-gather.5.cloned.1.call-update) | async-done | bytes 10616848 | tf_op jit(solution)/shard_map/all_gather | solution.py:82
  515.7 6.0 %convert_multiply_fusion = f32[5184,8,128]{2,1,0:T(8,128)S(1)} fusion(bf16[5184,8,128]{2,1,0:T(8,128)(2,1)} %all-gather.5.cloned.1.call-done), kind=kLoop, calls=%fused_computation.4 | loop fusion | flops 10616832 | bytes 31850496 | tf_op jit(solution)/shard_map/mul | solution.py:84
  521.8 15.7 %fusion.1 = f32[12,576,768]{2,1,0:T(8,128)} fusion(f32[12,576,768]{2,1,0:T(8,128)} %param.3, f32[12,576,768]{2,1,0:T(8,128)S(1)} %bitcast.82), kind=kLoop, calls=%fused_computation.2 | loop fusion | flops 21233664 | bytes 63700992 | tf_op jit(solution)/shard_map/sub | solution.py:84
Async XLA Ops:
  7.2 255.9 %reduce-scatter.4.cloned.1.call-start = ((), (), s32[]{:S(2)}) async-start(), calls=%async_computation.3 | async-start | bytes 21565440
  18.8 364.4 %all-gather.3.cloned.1.call-start = ((), (), s32[]{:S(2)}) async-start(), calls=%async_computation.1 | async-start | bytes 21565440 | tf_op jit(solution)/shard_map/all_gather | solution.py:52
  264.8 250.9 %all-gather.5.cloned.1.call-start = ((), (), s32[]{:S(2)}) async-start(), calls=%async_computation.2 | async-start | bytes 10782720 | tf_op jit(solution)/shard_map/all_gather | solution.py:82
  385.5 4.3 collective-permute-start
  395.2 1.2 copy-start
  428.2 2.5 collective-permute-start.1
Sparse Core Ops, SparseCore 0:
  18.9 244.0 reduce-scatter.3
  266.4 116.7 all-gather.2
  431.9 83.8 all-gather.4

commit v2 on v0

v2 whole, which is shorter than its diff:
```python
import functools
import math
import jax
import jax.numpy as jnp
from jax import lax
from jax.experimental import pallas as pl
from jax.experimental.pallas import tpu as pltpu
from jax.sharding import PartitionSpec as P

MOMENTUM = 0.95
LEARN_RATE = 0.25
WEIGHT_DECAY = 0.1
COEF_A = 3.4445
COEF_B = -4.7750
COEF_C = 2.0315
NORM_EPS = 1e-7
NS_STEPS = 5

MESH = pl.DeviceIdType.MESH
SIDE = 4
PARTS = 3
STRIDES = (1, 4, 16)
KINDS = 6
PHASES = 6
SWAPS = 4


def dot_nn(lhs, rhs):
    return lax.dot_general(lhs, rhs, (((1,), (0,)), ((), ())), preferred_element_type=jnp.float32)


def dot_nt(lhs, rhs):
    return lax.dot_general(lhs, rhs, (((1,), (1,)), ((), ())), preferred_element_type=jnp.float32)


def kernel(rows, cols, data_size, grad_ref, mom_ref, mean_ref, ortho_ref, raw_in, raw_relay, raw_own, sum_line, line_in,
           line_relay, plane, mean_own, mom_own, nest, nest_in, x_buf, gram_buf, poly_buf, x_half, send_sem, recv_sem,
           local_sem):
    data_idx = lax.axis_index("data")
    tp_idx = lax.axis_index("tp")
    partner = {"tp": 1 - tp_idx}
    half = rows // 2
    quarter = rows // SIDE
    eighth = quarter // 2

    coord, plus, minus = [], [], []
    for stride in STRIDES:
        here = lax.rem(lax.div(data_idx, stride), SIDE)
        coord.append(here)
        plus.append({"data": data_idx + (lax.rem(here + 1, SIDE) - here) * stride})
        minus.append({"data": data_idx + (lax.rem(here + SIDE - 1, SIDE) - here) * stride})

    def step_of(axis, distance):
        return lax.rem(coord[axis] + distance, SIDE)

    def axes_of(part):
        return part, (part + 1) % PARTS, (part + 2) % PARTS

    def remote(src, dst, index, device):
        return pltpu.make_async_remote_copy(src_ref=src, dst_ref=dst, send_sem=send_sem.at[index],
                                            recv_sem=recv_sem.at[index], device_id=device, device_id_type=MESH)

    def base_of(phase, part):
        return (phase * PARTS + part) * KINDS

    def local(src, dst, index):
        return pltpu.make_async_copy(src, dst, local_sem.at[index])

    def spread(phase, part, axis, block, height, relay, landing):
        base = base_of(phase, part)
        mid = height // 2
        far = step_of(axis, 2)
        return [
            remote(block(far, 0, mid), relay.at[0], base + 0, plus[axis]),
            remote(block(far, mid, mid), relay.at[1], base + 1, minus[axis]),
            remote(block(step_of(axis, 1), 0, height), landing.at[0], base + 2, plus[axis]),
            remote(block(step_of(axis, 3), 0, height), landing.at[1], base + 3, minus[axis]),
            remote(relay.at[0], landing.at[2, pl.ds(0, mid)], base + 4, plus[axis]),
            remote(relay.at[1], landing.at[2, pl.ds(mid, mid)], base + 5, minus[axis]),
        ]

    def gather(phase, part, axis, own, slot):
        base = base_of(phase, part)
        here = coord[axis]
        left, right = step_of(axis, 3), step_of(axis, 1)
        return [
            remote(own(0), slot(here, 0), base + 0, plus[axis]),
            remote(own(1), slot(here, 1), base + 1, minus[axis]),
            remote(own(1), slot(here, 1), base + 2, plus[axis]),
            remote(own(0), slot(here, 0), base + 3, minus[axis]),
            remote(slot(left, 0), slot(left, 0), base + 4, plus[axis]),
            remote(slot(right, 1), slot(right, 1), base + 5, minus[axis]),
        ]

    def launch(copies):
        for copy in copies[:4]:
            copy.start()

    def forward(copies):
        copies[0].wait_recv()
        copies[4].start()
        copies[1].wait_recv()
        copies[5].start()

    def arrive(copies):
        for copy in copies[2:]:
            copy.wait_recv()

    def over_rows(count, chunk, body):
        def run(index, carry):
            body(pl.ds(pl.multiple_of(index * chunk, chunk), chunk))
            return carry
        lax.fori_loop(0, count // chunk, run, 0)

    fetch_raw, fetch_mom = [], []
    for part in range(PARTS):
        mine = part * SIDE + step_of(part, 0)
        fetch_raw.append(local(grad_ref.at[mine], raw_own.at[part], part))
        fetch_mom.append(local(mom_ref.at[mine], mom_own.at[part], PARTS + part))
    for fetch in fetch_raw + fetch_mom:
        fetch.start()

    barrier = pltpu.get_barrier_semaphore()
    for device in plus + minus + [partner]:
        pl.semaphore_signal(barrier, inc=1, device_id=device, device_id_type=MESH)
    pl.semaphore_wait(barrier, 2 * PARTS + 1)

    copies1, copies2, copies3, copies4, copies5, copies6 = [], [], [], [], [], []
    for part in range(PARTS):
        copies1.append(spread(0, part, part, lambda j, at, size, part=part: grad_ref.at[part * SIDE + j, pl.ds(at, size)],
                              rows, raw_relay.at[part], raw_in.at[part]))
        launch(copies1[part])
    for part in range(PARTS):
        forward(copies1[part])

    for part in range(PARTS):
        fetch_raw[part].wait()
        arrive(copies1[part])

        def add_line(at, part=part):
            total = raw_own[part, at].astype(jnp.float32) + raw_in[part, 0, at].astype(jnp.float32)
            total = total + raw_in[part, 1, at].astype(jnp.float32)
            sum_line[part, at] = total + raw_in[part, 2, at].astype(jnp.float32)

        over_rows(rows, 16, add_line)
        axis = axes_of(part)[1]

        def quarter_block(j, at, size, part=part):
            return sum_line.at[part, pl.ds(pl.multiple_of(j * quarter + at, 8), size)]

        copies2.append(spread(1, part, axis, quarter_block, quarter, line_relay.at[part], line_in.at[part]))
        launch(copies2[part])
    for part in range(PARTS):
        forward(copies2[part])

    for part in range(PARTS):
        arrive(copies2[part])
        axis_b, axis_c = axes_of(part)[1:]

        def add_plane(at, part=part, axis_b=axis_b, axis_c=axis_c):
            own_at = pl.ds(pl.multiple_of(coord[axis_b] * quarter + at.start, 8), at.size)
            plane[part, coord[axis_c], at] = (sum_line[part, own_at] + line_in[part, 0, at]) + (
                line_in[part, 1, at] + line_in[part, 2, at])

        over_rows(quarter, 16, add_plane)

        def plane_slot(slot, which, part=part):
            return plane.at[part, slot, pl.ds(which * eighth, eighth)]

        copies3.append(gather(2, part, axis_c, lambda which, slot=plane_slot, axis=axis_c: slot(coord[axis], which), plane_slot))
        launch(copies3[part])
    for part in range(PARTS):
        forward(copies3[part])

    for part in range(PARTS):
        arrive(copies3[part])
        axis_b = axes_of(part)[1]

        def add_cube(at, part=part, axis_b=axis_b):
            own_at = pl.ds(pl.multiple_of(coord[axis_b] * quarter + at.start, 8), at.size)
            total = (plane[part, 0, at] + plane[part, 1, at]) + (plane[part, 2, at] + plane[part, 3, at])
            mean_own[part, own_at] = total * (1.0 / data_size)

        over_rows(quarter, 16, add_cube)

        def mean_slot(slot, which, part=part):
            return mean_own.at[part, pl.ds(pl.multiple_of(slot * quarter + which * eighth, 8), eighth)]

        copies4.append(gather(3, part, axis_b, lambda which, slot=mean_slot, axis=axis_b: slot(coord[axis], which), mean_slot))
        launch(copies4[part])
    for part in range(PARTS):
        forward(copies4[part])

    for part in range(PARTS):
        arrive(copies4[part])
        mine = part * SIDE + step_of(part, 0)

        def out_slot(slot, which, part=part):
            return mean_ref.at[part * SIDE + slot, pl.ds(which * half, half)]

        copies5.append(gather(4, part, part, lambda which, part=part: mean_own.at[part, pl.ds(which * half, half)], out_slot))
        launch(copies5[part])
        local(mean_own.at[part], mean_ref.at[mine], 2 * PARTS + part).start()

    swap_base = PHASES * PARTS * KINDS
    for part in range(PARTS):
        fetch_mom[part].wait()

        def nesterov(at, part=part):
            mean = mean_own[part, at]
            nest[part, at] = mean + MOMENTUM * (MOMENTUM * mom_own[part, at] + mean)

        over_rows(rows, 16, nesterov)
    give_first = remote(nest.at[1 - tp_idx], nest_in.at[0], swap_base, partner)
    give_first.start()
    give_second = remote(nest.at[2], nest_in.at[1], swap_base + 1, partner)

    @pl.when(tp_idx == 1)
    def _():
        give_second.start()

    def orthogonalise(part, which):
        def squares(index, total):
            at = pl.ds(pl.multiple_of(index * 8, 8), 8)
            own, other = nest[part, at], nest_in[which, at]
            return total + (own * own + other * other)

        total = lax.fori_loop(0, rows // 8, squares, jnp.zeros((8, cols), jnp.float32))
        scale = 1.0 / (jnp.sqrt(jnp.sum(total, keepdims=True)) + NORM_EPS)

        def normalise(at):
            x_buf[0, at, pl.ds(0, cols)] = (nest[part, at] * scale).astype(jnp.bfloat16)
            x_buf[0, at, pl.ds(cols, cols)] = (nest_in[which, at] * scale).astype(jnp.bfloat16)

        over_rows(rows, 16, normalise)

        def newton(step, carry):
            now = lax.rem(step, 2)
            later = 1 - now
            gram_buf[...] = dot_nt(x_buf[now], x_buf[now]).astype(jnp.bfloat16)
            square = dot_nn(gram_buf[...], gram_buf[...])
            poly_buf[...] = (COEF_B * gram_buf[...].astype(jnp.float32) + COEF_C * square).astype(jnp.bfloat16)
            for at in range(0, 2 * cols, cols // 3):
                strip = x_buf[now, :, pl.ds(at, cols // 3)]
                update = dot_nn(poly_buf[...], strip)
                x_buf[later, :, pl.ds(at, cols // 3)] = (COEF_A * strip.astype(jnp.float32) + update).astype(jnp.bfloat16)
            return carry

        lax.fori_loop(0, NS_STEPS, newton, 0)

    final = NS_STEPS % 2

    def keep_half(part):
        def move(at):
            x_half[part, at] = x_buf[final, at, pl.ds(0, cols)]
        over_rows(rows, 16, move)

    give_first.wait_recv()
    orthogonalise(tp_idx, 0)
    swap_x = remote(x_buf.at[final, :, pl.ds(cols, cols)], x_half.at[tp_idx], swap_base + 2, partner)
    swap_x.start()
    for part in range(PARTS):
        forward(copies5[part])
    keep_half(tp_idx)
    swap_x.wait()

    def ortho_gather(part):
        mine = part * SIDE + step_of(part, 0)

        def slot(index, which):
            return ortho_ref.at[part * SIDE + index, pl.ds(which * half, half)]

        copies = gather(5, part, part, lambda which: x_half.at[part, pl.ds(which * half, half)], slot)
        launch(copies)
        local(x_half.at[part], ortho_ref.at[mine], 3 * PARTS + part).start()
        return copies

    copies6.append(ortho_gather(0))
    copies6.append(ortho_gather(1))

    give_x = remote(x_buf.at[final, :, pl.ds(cols, cols)], x_half.at[2], swap_base + 3, partner)

    @pl.when(tp_idx == 0)
    def _():
        give_second.wait_recv()
        orthogonalise(2, 1)
        give_x.start()
        keep_half(2)
        give_x.wait_send()

    @pl.when(tp_idx == 1)
    def _():
        forward(copies6[0])
        forward(copies6[1])
        give_x.wait_recv()
        give_second.wait_send()

    copies6.append(ortho_gather(2))

    @pl.when(tp_idx == 0)
    def _():
        forward(copies6[0])
        forward(copies6[1])

    forward(copies6[2])
    for part in range(PARTS):
        arrive(copies5[part])
        arrive(copies6[part])
        mine = part * SIDE + step_of(part, 0)
        local(mean_own.at[part], mean_ref.at[mine], 2 * PARTS + part).wait()
        local(x_half.at[part], ortho_ref.at[mine], 3 * PARTS + part).wait()
    give_first.wait_send()
    for copies in copies1 + copies2 + copies3 + copies4 + copies5 + copies6:
        for copy in copies:
            copy.wait_send()


def solution(mesh):
    data_size = mesh.shape["data"]
    tp_size = mesh.shape["tp"]
    state_spec = P("stage", None, "tp")
    grad_spec = P("stage", "data", None, "tp")

    def per_device(weight, momentum, grad):
        layers, rows, cols = weight.shape
        quarter = rows // SIDE
        copies = PHASES * PARTS * KINDS + SWAPS
        bf16, f32 = jnp.bfloat16, jnp.float32
        mean, ortho = pl.pallas_call(
            functools.partial(kernel, rows, cols, data_size),
            out_shape=(jax.ShapeDtypeStruct((layers, rows, cols), f32), jax.ShapeDtypeStruct((layers, rows, cols), bf16)),
            in_specs=[pl.BlockSpec(memory_space=pl.ANY)] * 2,
            out_specs=(pl.BlockSpec(memory_space=pl.ANY),) * 2,
            scratch_shapes=[
                pltpu.VMEM((PARTS, 3, rows, cols), bf16),
                pltpu.VMEM((PARTS, 2, rows // 2, cols), bf16),
                pltpu.VMEM((PARTS, rows, cols), bf16),
                pltpu.VMEM((PARTS, rows, cols), f32),
                pltpu.VMEM((PARTS, 3, quarter, cols), f32),
                pltpu.VMEM((PARTS, 2, quarter // 2, cols), f32),
                pltpu.VMEM((PARTS, SIDE, quarter, cols), f32),
                pltpu.VMEM((PARTS, rows, cols), f32),
                pltpu.VMEM((PARTS, rows, cols), f32),
                pltpu.VMEM((PARTS, rows, cols), f32),
                pltpu.VMEM((2, rows, cols), f32),
                pltpu.VMEM((2, rows, tp_size * cols), bf16),
                pltpu.VMEM((rows, rows), bf16),
                pltpu.VMEM((rows, rows), bf16),
                pltpu.VMEM((PARTS, rows, cols), bf16),
                pltpu.SemaphoreType.DMA((copies,)),
                pltpu.SemaphoreType.DMA((copies,)),
                pltpu.SemaphoreType.DMA((4 * PARTS,)),
            ],
            compiler_params=pltpu.CompilerParams(collective_id=0, has_side_effects=True, vmem_limit_bytes=67043328),
        )(grad.reshape(layers, rows, cols), momentum)
        new_mom = MOMENTUM * momentum + mean
        rms_scale = 0.2 * math.sqrt(max(rows, cols * tp_size))
        new_weight = weight - LEARN_RATE * (rms_scale * ortho.astype(f32) + WEIGHT_DECAY * weight)
        return new_weight, new_mom

    return jax.shard_map(per_device, mesh=mesh, in_specs=(state_spec, state_spec, grad_spec), out_specs=(state_spec, state_spec), check_vma=False)
```

time: 809 us -> 229 us (0.28)
  matrix products: 249 us -> 0 us
  blocking collectives: 248 us -> 0 us
  waiting for transfers between devices: 242 us -> 0 us
  Pallas kernels: 0 us -> 189 us
  between operations: 14.3 us -> 0.64 us
  other arithmetic: 51.3 us -> 39.2 us
    dot_general x10 -> x0, matrix products: 249 us -> none  [the longest x5 160 us: per_device(): jnp.einsum('lij,ljk->lik', poly_mat, ortho, preferred_element_type=jnp.fl...]
    psum x6 -> x0, blocking collectives: 248 us -> none  [the longest x5 244 us: per_device(): gram_mat = lax.psum(part_gram, 'tp').astype(jnp.bfloat16)]
    psum x1 -> x0, waiting for transfers between devices: 242 us -> none  [per_device(): grad_mean = lax.psum(grad_sum, 'data') / data_size]
    pallas_call x0 -> x1, Pallas kernels: none -> 189 us  [per_device(): pl.pallas_call(functools.partial(kernel, rows, cols, data_size), out_shap...]
    add x0 -> x1, other arithmetic: none -> 39.2 us  [per_device(): new_mom = MOMENTUM * momentum + mean]
    reduce_sum x2 -> x0, other arithmetic: 33 us -> none  [the longest x1 21.4 us: per_device(): square_part = jnp.sum(nesterov * nesterov, axis=(1, 2), keepdims=True)]
    convert_element_type x1 -> x0, other arithmetic: 18.2 us -> none  [per_device(): ortho = (nesterov / (norms + NORM_EPS)).astype(jnp.bfloat16)]
  transfers between devices with their start and end apart: 1 -> 0, of which waited for: 1 -> 0; matrix products, arithmetic and copies ran while one was open for 0% -> 0% of each run, Pallas kernels for 0% -> 0%
where the time goes in v2:
time: 229 us
  Pallas kernels  189 us (83%)
  other arithmetic  39.2 us (17%)
    pallas_call x1, Pallas kernels, per_device(): pl.pallas_call(functools.partial(kernel, rows, cols, data_size), out_shap...  189 us
    add x1, other arithmetic, per_device(): new_mom = MOMENTUM * momentum + mean  39.2 us

profile of v2, /device:TPU:1, one launch (start us, length us, event | category | flops | bytes accessed | tf_op | source)
XLA Modules:
  0.0 228.6 jit_solution(5844040472133392572)
XLA Ops:
  0.6 188.8 %shard_map.50 = (f32[12,576,768]{2,1,0:T(8,128)}, bf16[12,576,768]{2,1,0:T(8,128)(2,1)}) custom-call(bf16[12,576,768]{2,1,0:T(8,128)(2,1)} %bitcast.1, f32[12,576,768]{2,1,0:T(8,128)} %mom_ref.1), custom_call_target="tpu_custom_call" | custom-call | tf_op jit(solution)/shard_map/pallas_call | solution.py:329
  189.5 39.2 %multiply_add_fusion = (f32[12,576,768]{2,1,0:T(8,128)}, f32[12,576,768]{2,1,0:T(8,128)}) fusion(f32[12,576,768]{2,1,0:T(8,128)} %get-tuple-element.5, f32[12,576,768]{2,1,0:T(8,128)} %mom_ref.1, f32[12,576,768]{2,1,0:T(8,128)} %param.3, bf16[12,576,768]{2,1,0:T(8,128)(2,1)} %get-tuple-element.4), kind=kLoop, calls=%fused_computation | loop fusion | flops 42467328 | bytes 116785152 | tf_op jit(solution)/shard_map/add | solution.py:356

commit v3 on v2

v3 whole, which is shorter than its diff:
```python
import functools
import math
import jax
import jax.numpy as jnp
from jax import lax
from jax.experimental import pallas as pl
from jax.experimental.pallas import tpu as pltpu
from jax.sharding import PartitionSpec as P

MOMENTUM = 0.95
LEARN_RATE = 0.25
WEIGHT_DECAY = 0.1
COEF_A = 3.4445
COEF_B = -4.7750
COEF_C = 2.0315
NORM_EPS = 1e-7
NS_STEPS = 5

MESH = pl.DeviceIdType.MESH
SIDE = 4
PARTS = 3
STRIDES = (1, 4, 16)
KINDS = 6
PHASES = 6
SWAPS = 4
VMEM_KERNEL = 22 * 1024 * 1024
VMEM_FLUSH = 1024 * 1024
ORDER = (0, 3, 1, 2)


def dot_nn(lhs, rhs):
    return lax.dot_general(lhs, rhs, (((1,), (0,)), ((), ())), preferred_element_type=jnp.float32)


def dot_nt(lhs, rhs):
    return lax.dot_general(lhs, rhs, (((1,), (1,)), ((), ())), preferred_element_type=jnp.float32)


def kernel(rows, cols, data_size, rms_scale, grad_ref, mom_ref, weight_ref, held, ortho_all, x_buf, gram_buf, poly_buf,
           nest_in, send_sem, recv_sem, local_sem):
    data_idx = lax.axis_index("data")
    tp_idx = lax.axis_index("tp")
    partner = {"tp": 1 - tp_idx}
    half = rows // 2
    quarter = rows // SIDE
    eighth = quarter // 2
    layers = PARTS * SIDE
    mom_out = held.at[pl.ds(0, layers)]
    weight_out = held.at[pl.ds(layers, layers)]

    def raw_in(part, slot):
        return ortho_all.at[part * 3 + slot]

    def raw_relay(part, way):
        return ortho_all.at[3 * PARTS + part, pl.ds(way * half, half)]

    def raw_own(part):
        return x_buf.at[part // 2, :, pl.ds(part % 2 * cols, cols)]

    def sum_line(part):
        return weight_out.at[part]

    def line_in(part, slot):
        return weight_out.at[PARTS + part, pl.ds(slot * quarter, quarter)]

    def line_relay(part, way):
        return weight_out.at[PARTS + part, pl.ds(3 * quarter + way * eighth, eighth)]

    def plane(part, slot):
        return weight_out.at[2 * PARTS + part, pl.ds(pl.multiple_of(slot * quarter, 8), quarter)]

    def mom_own(part):
        return weight_out.at[3 * PARTS + part]

    def nest(part):
        return weight_out.at[part]

    coord, plus, minus = [], [], []
    for stride in STRIDES:
        here = lax.rem(lax.div(data_idx, stride), SIDE)
        coord.append(here)
        plus.append({"data": data_idx + (lax.rem(here + 1, SIDE) - here) * stride})
        minus.append({"data": data_idx + (lax.rem(here + SIDE - 1, SIDE) - here) * stride})

    def step_of(axis, distance):
        return lax.rem(coord[axis] + distance, SIDE)

    def layer_of(part, distance):
        return part * SIDE + step_of(part, distance)

    def axes_of(part):
        return part, (part + 1) % PARTS, (part + 2) % PARTS

    def remote(src, dst, index, device):
        return pltpu.make_async_remote_copy(src_ref=src, dst_ref=dst, send_sem=send_sem.at[index],
                                            recv_sem=recv_sem.at[index], device_id=device, device_id_type=MESH)

    def base_of(phase, part):
        return (phase * PARTS + part) * KINDS

    def local(src, dst, index):
        return pltpu.make_async_copy(src, dst, local_sem.at[index])

    def spread(phase, part, axis, block, height, relay, landing):
        base = base_of(phase, part)
        mid = height // 2
        far = step_of(axis, 2)
        return [
            remote(block(far, 0, mid), relay(part, 0), base + 0, plus[axis]),
            remote(block(far, mid, mid), relay(part, 1), base + 1, minus[axis]),
            remote(block(step_of(axis, 1), 0, height), landing(part, 0), base + 2, plus[axis]),
            remote(block(step_of(axis, 3), 0, height), landing(part, 1), base + 3, minus[axis]),
            remote(relay(part, 0), landing(part, 2).at[pl.ds(0, mid)], base + 4, plus[axis]),
            remote(relay(part, 1), landing(part, 2).at[pl.ds(mid, mid)], base + 5, minus[axis]),
        ]

    def gather(phase, part, axis, slot):
        base = base_of(phase, part)
        here = coord[axis]
        left, right = step_of(axis, 3), step_of(axis, 1)
        return [
            remote(slot(here, 0), slot(here, 0), base + 0, plus[axis]),
            remote(slot(here, 1), slot(here, 1), base + 1, minus[axis]),
            remote(slot(here, 1), slot(here, 1), base + 2, plus[axis]),
            remote(slot(here, 0), slot(here, 0), base + 3, minus[axis]),
            remote(slot(left, 0), slot(left, 0), base + 4, plus[axis]),
            remote(slot(right, 1), slot(right, 1), base + 5, minus[axis]),
        ]

    def launch(copies):
        for copy in copies[:4]:
            copy.start()

    def forward(copies):
        copies[0].wait_recv()
        copies[4].start()
        copies[1].wait_recv()
        copies[5].start()

    def arrive(copies):
        for copy in copies[2:]:
            copy.wait_recv()

    def sent(copies):
        for copy in copies:
            copy.wait_send()

    def over_rows(count, chunk, body):
        def run(index, carry):
            body(pl.ds(pl.multiple_of(index * chunk, chunk), chunk))
            return carry
        lax.fori_loop(0, count // chunk, run, 0)

    fetch_raw, fetch_mom = [], []
    for part in range(PARTS):
        fetch_raw.append(local(grad_ref.at[layer_of(part, 0)], raw_own(part), part))
        fetch_mom.append(local(mom_ref.at[layer_of(part, 0)], mom_own(part), PARTS + part))
    for fetch in fetch_raw + fetch_mom:
        fetch.start()

    barrier = pltpu.get_barrier_semaphore()
    for device in plus + minus + [partner]:
        pl.semaphore_signal(barrier, inc=1, device_id=device, device_id_type=MESH)
    pl.semaphore_wait(barrier, 2 * PARTS + 1)

    copies1, copies2, copies3, copies4, copies5, copies6 = [], [], [], [], [], []
    for part in range(PARTS):
        def raw_block(j, at, size, part=part):
            return grad_ref.at[part * SIDE + j, pl.ds(at, size)]

        copies1.append(spread(0, part, part, raw_block, rows, raw_relay, raw_in))
        launch(copies1[part])
    for part in range(PARTS):
        forward(copies1[part])

    for part in range(PARTS):
        fetch_raw[part].wait()
        arrive(copies1[part])

        def add_line(at, part=part):
            total = raw_own(part)[at].astype(jnp.float32) + raw_in(part, 0)[at].astype(jnp.float32)
            total = total + raw_in(part, 1)[at].astype(jnp.float32)
            sum_line(part)[at] = total + raw_in(part, 2)[at].astype(jnp.float32)

        over_rows(rows, 16, add_line)

        def quarter_block(j, at, size, part=part):
            return sum_line(part).at[pl.ds(pl.multiple_of(j * quarter + at, 8), size)]

        copies2.append(spread(1, part, axes_of(part)[1], quarter_block, quarter, line_relay, line_in))
        launch(copies2[part])
    for part in range(PARTS):
        forward(copies2[part])

    for part in range(PARTS):
        arrive(copies2[part])
        axis_b, axis_c = axes_of(part)[1:]

        def add_plane(at, part=part, axis_b=axis_b, axis_c=axis_c):
            own_at = pl.ds(pl.multiple_of(coord[axis_b] * quarter + at.start, 8), at.size)
            plane(part, coord[axis_c])[at] = (sum_line(part)[own_at] + line_in(part, 0)[at]) + (
                line_in(part, 1)[at] + line_in(part, 2)[at])

        over_rows(quarter, 16, add_plane)

        def plane_slot(slot, which, part=part):
            return plane(part, slot).at[pl.ds(which * eighth, eighth)]

        copies3.append(gather(2, part, axis_c, plane_slot))
        launch(copies3[part])
    for part in range(PARTS):
        forward(copies3[part])

    for part in range(PARTS):
        arrive(copies3[part])
        axis_b = axes_of(part)[1]

        def add_cube(at, part=part, axis_b=axis_b):
            own_at = pl.ds(pl.multiple_of(coord[axis_b] * quarter + at.start, 8), at.size)
            total = (plane(part, 0)[at] + plane(part, 1)[at]) + (plane(part, 2)[at] + plane(part, 3)[at])
            mom_out[layer_of(part, 0), own_at] = total * (1.0 / data_size)

        over_rows(quarter, 16, add_cube)

        def mean_slot(slot, which, part=part):
            return mom_out.at[layer_of(part, 0), pl.ds(pl.multiple_of(slot * quarter + which * eighth, 8), eighth)]

        copies4.append(gather(3, part, axis_b, mean_slot))
        launch(copies4[part])
    for part in range(PARTS):
        forward(copies4[part])
    for part in range(PARTS):
        sent(copies1[part])
        sent(copies2[part])
        sent(copies3[part])

    for part in range(PARTS):
        arrive(copies4[part])

        def mean_block(slot, which, part=part):
            return mom_out.at[part * SIDE + slot, pl.ds(which * half, half)]

        copies5.append(gather(4, part, part, mean_block))
        launch(copies5[part])

    swap_base = PHASES * PARTS * KINDS
    for part in range(PARTS):
        fetch_mom[part].wait()

        def nesterov(at, part=part):
            mean = mom_out[layer_of(part, 0), at]
            nest(part)[at] = mean + MOMENTUM * (MOMENTUM * mom_own(part)[at] + mean)

        over_rows(rows, 16, nesterov)
    give_first = remote(weight_out.at[1 - tp_idx], nest_in.at[0], swap_base, partner)
    give_first.start()
    give_second = remote(nest(2), nest_in.at[1], swap_base + 1, partner)

    @pl.when(tp_idx == 1)
    def _():
        give_second.start()

    weight_base = 2 * PARTS
    fetch_weight = [local(weight_ref.at[layer], weight_out.at[layer], weight_base + layer) for layer in range(layers)]
    for fetch in fetch_weight[PARTS:]:
        fetch.start()

    def orthogonalise(part, which):
        def squares(index, total):
            at = pl.ds(pl.multiple_of(index * 8, 8), 8)
            own, other = weight_out[part, at], nest_in[which, at]
            return total + (own * own + other * other)

        total = lax.fori_loop(0, rows // 8, squares, jnp.zeros((8, cols), jnp.float32))
        scale = 1.0 / (jnp.sqrt(jnp.sum(total, keepdims=True)) + NORM_EPS)

        def normalise(at):
            x_buf[0, at, pl.ds(0, cols)] = (weight_out[part, at] * scale).astype(jnp.bfloat16)
            x_buf[0, at, pl.ds(cols, cols)] = (nest_in[which, at] * scale).astype(jnp.bfloat16)

        over_rows(rows, 16, normalise)

        def newton(step, carry):
            now = lax.rem(step, 2)
            later = 1 - now
            gram_buf[...] = dot_nt(x_buf[now], x_buf[now]).astype(jnp.bfloat16)
            square = dot_nn(gram_buf[...], gram_buf[...])
            poly_buf[...] = (COEF_B * gram_buf[...].astype(jnp.float32) + COEF_C * square).astype(jnp.bfloat16)
            for at in range(0, 2 * cols, cols // 3):
                strip = x_buf[now, :, pl.ds(at, cols // 3)]
                update = dot_nn(poly_buf[...], strip)
                x_buf[later, :, pl.ds(at, cols // 3)] = (COEF_A * strip.astype(jnp.float32) + update).astype(jnp.bfloat16)
            return carry

        lax.fori_loop(0, NS_STEPS, newton, 0)

    final = NS_STEPS % 2
    first_layer = jnp.where(tp_idx == 0, layer_of(0, 0), layer_of(1, 0))

    def keep_half(layer):
        def move(at):
            ortho_all[layer, at] = x_buf[final, at, pl.ds(0, cols)]
        over_rows(rows, 16, move)

    def ortho_gather(part):
        def slot(index, which):
            return ortho_all.at[part * SIDE + index, pl.ds(which * half, half)]

        copies6.append(gather(5, part, part, slot))
        launch(copies6[part])

    give_first.wait_recv()
    orthogonalise(tp_idx, 0)
    swap_x = remote(x_buf.at[final, :, pl.ds(cols, cols)], ortho_all.at[first_layer], swap_base + 2, partner)
    swap_x.start()
    for part in range(PARTS):
        forward(copies5[part])
    keep_half(first_layer)
    swap_x.wait()
    ortho_gather(0)
    ortho_gather(1)

    give_x = remote(x_buf.at[final, :, pl.ds(cols, cols)], ortho_all.at[layer_of(2, 0)], swap_base + 3, partner)

    @pl.when(tp_idx == 0)
    def _():
        give_second.wait_recv()
        orthogonalise(2, 1)
        give_x.start()
        keep_half(layer_of(2, 0))
        give_x.wait_send()

    @pl.when(tp_idx == 1)
    def _():
        give_x.wait_recv()
        give_second.wait_send()

    ortho_gather(2)
    give_first.wait_send()
    for fetch in fetch_weight[:PARTS]:
        fetch.start()

    stream_base = weight_base + layers
    turns = [(part, distance) for distance in ORDER for part in range(PARTS)]
    fetch_turn = [local(mom_ref.at[layer_of(*turn)], nest_in.at[index % 2], stream_base + index)
                  for index, turn in enumerate(turns)]
    fetch_turn[0].start()
    fetch_turn[1].start()
    for index, (part, distance) in enumerate(turns):
        if distance == 0:
            sent(copies4[part])
            sent(copies5[part][:4])
        elif distance == 3:
            copies5[part][2].wait_recv()
            copies5[part][4].wait_send()
        elif distance == 1:
            copies5[part][3].wait_recv()
            copies5[part][5].wait_send()
        else:
            copies5[part][4].wait_recv()
            copies5[part][5].wait_recv()
        fetch_turn[index].wait()
        layer = layer_of(part, distance)

        def momentum(at, layer=layer, index=index):
            mom_out[layer, at] = MOMENTUM * nest_in[index % 2, at] + mom_out[layer, at]

        over_rows(rows, 16, momentum)
        if index + 2 < len(turns):
            fetch_turn[index + 2].start()

    for part in range(PARTS):
        forward(copies6[part])
    for fetch in fetch_weight:
        fetch.wait()
    for part, distance in turns:
        if distance == 3:
            copies6[part][2].wait_recv()
        elif distance == 1:
            copies6[part][3].wait_recv()
        elif distance == 2:
            copies6[part][4].wait_recv()
            copies6[part][5].wait_recv()
        layer = layer_of(part, distance)

        def descend(at, layer=layer):
            weight = weight_out[layer, at]
            ortho = ortho_all[layer, at].astype(jnp.float32)
            weight_out[layer, at] = weight - LEARN_RATE * (rms_scale * ortho + WEIGHT_DECAY * weight)

        over_rows(rows, 16, descend)
    for part in range(PARTS):
        sent(copies6[part])


def flush(held, mom_ref, weight_ref, sem):
    layers = mom_ref.shape[0]
    copies = []
    for layer in range(layers):
        copies.append(pltpu.make_async_copy(held.at[layer], mom_ref.at[layer], sem.at[layer]))
        copies.append(pltpu.make_async_copy(held.at[layers + layer], weight_ref.at[layer], sem.at[layers + layer]))
    for copy in copies:
        copy.start()
    for copy in copies:
        copy.wait()


def solution(mesh):
    data_size = mesh.shape["data"]
    tp_size = mesh.shape["tp"]
    state_spec = P("stage", None, "tp")
    grad_spec = P("stage", "data", None, "tp")

    def per_device(weight, momentum, grad):
        layers, rows, cols = weight.shape
        copies = PHASES * PARTS * KINDS + SWAPS
        rms_scale = 0.2 * math.sqrt(max(rows, cols * tp_size))
        bf16, f32 = jnp.bfloat16, jnp.float32
        in_hbm = pl.BlockSpec(memory_space=pltpu.HBM)
        in_vmem = pl.BlockSpec(memory_space=pltpu.VMEM)
        held = pl.pallas_call(
            functools.partial(kernel, rows, cols, data_size, rms_scale),
            out_shape=pltpu.VMEM((2 * layers, rows, cols), f32),
            in_specs=[in_hbm] * 3,
            out_specs=in_vmem,
            scratch_shapes=[
                pltpu.VMEM((layers, rows, cols), bf16),
                pltpu.VMEM((2, rows, tp_size * cols), bf16),
                pltpu.VMEM((rows, rows), bf16),
                pltpu.VMEM((rows, rows), bf16),
                pltpu.VMEM((2, rows, cols), f32),
                pltpu.SemaphoreType.DMA((copies,)),
                pltpu.SemaphoreType.DMA((copies,)),
                pltpu.SemaphoreType.DMA((2 * PARTS + 2 * layers,)),
            ],
            compiler_params=pltpu.CompilerParams(collective_id=0, has_side_effects=True, vmem_limit_bytes=VMEM_KERNEL),
        )(grad.reshape(layers, rows, cols), momentum, weight)
        new_mom, new_weight = pl.pallas_call(
            flush,
            out_shape=(jax.ShapeDtypeStruct((layers, rows, cols), f32),) * 2,
            in_specs=[in_vmem],
            out_specs=(in_hbm,) * 2,
            scratch_shapes=[pltpu.SemaphoreType.DMA((2 * layers,))],
            compiler_params=pltpu.CompilerParams(vmem_limit_bytes=VMEM_FLUSH),
        )(held)
        return new_weight, new_mom

    return jax.shard_map(per_device, mesh=mesh, in_specs=(state_spec, state_spec, grad_spec), out_specs=(state_spec, state_spec), check_vma=False)
```

time: 229 us -> 204 us (0.89)
  other arithmetic: 39.2 us -> 0 us
  Pallas kernels: 189 us -> 202 us
    add x1 -> x0, other arithmetic: 39.2 us -> none  [per_device(): new_mom = MOMENTUM * momentum + mean]
    pallas_call x1 -> x2, Pallas kernels: 189 us -> 202 us  [the longest x1 188 us: per_device(): pl.pallas_call(functools.partial(kernel, rows, cols, data_size, rms_scale...]
where the time goes in v3:
time: 204 us; the launch traced here: 202 us
  Pallas kernels  202 us (99%)
    pallas_call x1, Pallas kernels, per_device(): pl.pallas_call(functools.partial(kernel, rows, cols, data_size, rms_scale...  188 us
    pallas_call x1, Pallas kernels, per_device(): pl.pallas_call(flush, out_shape=(jax.ShapeDtypeStruct((layers, rows, cols...  13.8 us

profile of v3, /device:TPU:1, one launch (start us, length us, event | category | flops | bytes accessed | tf_op | source)
XLA Modules:
  0.0 202.2 jit_solution(9208842207262174906)
XLA Ops:
  0.6 187.8 %shard_map.50.held = f32[24,576,768]{2,1,0:T(8,128)S(1)} custom-call(bf16[12,576,768]{2,1,0:T(8,128)(2,1)} %bitcast.1, f32[12,576,768]{2,1,0:T(8,128)} %mom_ref.1, f32[12,576,768]{2,1,0:T(8,128)} %weight_ref.1), custom_call_target="tpu_custom_call" | custom-call | tf_op jit(solution)/shard_map/pallas_call | solution.py:421
  188.4 13.8 %shard_map.51 = (f32[12,576,768]{2,1,0:T(8,128)}, f32[12,576,768]{2,1,0:T(8,128)}) custom-call(f32[24,576,768]{2,1,0:T(8,128)S(1)} %shard_map.50.held), custom_call_target="tpu_custom_call" | custom-call | tf_op jit(solution)/shard_map/pallas_call | solution.py:438

commit v4 on v3

--- a/solution.py
+++ b/solution.py
@@ -22,6 +22,7 @@
 STRIDES = (1, 4, 16)
 KINDS = 6
 PHASES = 6
+CHUNKS = 2
 SWAPS = 4
 VMEM_KERNEL = 22 * 1024 * 1024
 VMEM_FLUSH = 1024 * 1024
@@ -48,26 +49,31 @@
     mom_out = held.at[pl.ds(0, layers)]
     weight_out = held.at[pl.ds(layers, layers)]
 
-    def raw_in(part, slot):
-        return ortho_all.at[part * 3 + slot]
-
-    def raw_relay(part, way):
-        return ortho_all.at[3 * PARTS + part, pl.ds(way * half, half)]
-
-    def raw_own(part):
-        return x_buf.at[part // 2, :, pl.ds(part % 2 * cols, cols)]
-
-    def sum_line(part):
-        return weight_out.at[part]
-
-    def line_in(part, slot):
-        return weight_out.at[PARTS + part, pl.ds(slot * quarter, quarter)]
-
-    def line_relay(part, way):
-        return weight_out.at[PARTS + part, pl.ds(3 * quarter + way * eighth, eighth)]
-
-    def plane(part, slot):
-        return weight_out.at[2 * PARTS + part, pl.ds(pl.multiple_of(slot * quarter, 8), quarter)]
+    width = cols // CHUNKS
+
+    def columns(chunk, start=0):
+        return pl.ds(start + chunk * width, width)
+
+    def raw_in(part, slot, chunk):
+        return ortho_all.at[part * 3 + slot, :, columns(chunk)]
+
+    def raw_relay(part, way, chunk):
+        return ortho_all.at[3 * PARTS + part, pl.ds(way * half, half), columns(chunk)]
+
+    def raw_own(part, chunk):
+        return x_buf.at[part // 2, :, columns(chunk, part % 2 * cols)]
+
+    def sum_line(part, chunk):
+        return weight_out.at[part, :, columns(chunk)]
+
+    def line_in(part, slot, chunk):
+        return weight_out.at[PARTS + part, pl.ds(slot * quarter, quarter), columns(chunk)]
+
+    def line_relay(part, way, chunk):
+        return weight_out.at[PARTS + part, pl.ds(2 * quarter + way * eighth, eighth), columns(chunk)]
+
+    def plane(part, slot, chunk):
+        return weight_out.at[2 * PARTS + part, pl.ds(pl.multiple_of(slot * quarter, 8), quarter), columns(chunk)]
 
     def mom_own(part):
         return weight_out.at[3 * PARTS + part]
@@ -95,27 +101,52 @@
         return pltpu.make_async_remote_copy(src_ref=src, dst_ref=dst, send_sem=send_sem.at[index],
                                             recv_sem=recv_sem.at[index], device_id=device, device_id_type=MESH)
 
-    def base_of(phase, part):
-        return (phase * PARTS + part) * KINDS
+    def base_of(phase, part, chunk=0):
+        return ((phase * CHUNKS + chunk) * PARTS + part) * KINDS
 
     def local(src, dst, index):
         return pltpu.make_async_copy(src, dst, local_sem.at[index])
 
-    def spread(phase, part, axis, block, height, relay, landing):
-        base = base_of(phase, part)
-        mid = height // 2
-        far = step_of(axis, 2)
+    def spread(part, chunk):
+        base = base_of(0, part, chunk)
+        far, right, left = layer_of(part, 2), layer_of(part, 1), layer_of(part, 3)
+
+        def block(layer, at, size):
+            return grad_ref.at[layer, pl.ds(at, size), columns(chunk)]
+
+        def landing(slot, at, size):
+            return raw_in(part, slot, chunk).at[pl.ds(at, size)]
+
         return [
-            remote(block(far, 0, mid), relay(part, 0), base + 0, plus[axis]),
-            remote(block(far, mid, mid), relay(part, 1), base + 1, minus[axis]),
-            remote(block(step_of(axis, 1), 0, height), landing(part, 0), base + 2, plus[axis]),
-            remote(block(step_of(axis, 3), 0, height), landing(part, 1), base + 3, minus[axis]),
-            remote(relay(part, 0), landing(part, 2).at[pl.ds(0, mid)], base + 4, plus[axis]),
-            remote(relay(part, 1), landing(part, 2).at[pl.ds(mid, mid)], base + 5, minus[axis]),
+            remote(block(far, 0, half), raw_relay(part, 0, chunk), base + 0, plus[part]),
+            remote(block(far, half, half), raw_relay(part, 1, chunk), base + 1, minus[part]),
+            remote(block(right, 0, rows), landing(0, 0, rows), base + 2, plus[part]),
+            remote(block(left, 0, rows), landing(1, 0, rows), base + 3, minus[part]),
+            remote(raw_relay(part, 0, chunk), landing(2, 0, half), base + 4, plus[part]),
+            remote(raw_relay(part, 1, chunk), landing(2, half, half), base + 5, minus[part]),
         ]
 
-    def gather(phase, part, axis, slot):
-        base = base_of(phase, part)
+    def line_block(part, distance, which, chunk):
+        at = step_of(axes_of(part)[1], distance) * quarter + which * eighth
+        return sum_line(part, chunk).at[pl.ds(pl.multiple_of(at, 8), eighth)]
+
+    def reduce(part, chunk):
+        base = base_of(1, part, chunk)
+        axis = axes_of(part)[1]
+
+        def landing(slot, which):
+            return line_in(part, slot, chunk).at[pl.ds(which * eighth, eighth)]
+
+        return [
+            remote(line_block(part, 2, 0, chunk), line_relay(part, 0, chunk), base + 0, plus[axis]),
+            remote(line_block(part, 2, 1, chunk), line_relay(part, 1, chunk), base + 1, minus[axis]),
+            remote(line_block(part, 1, 1, chunk), landing(0, 1), base + 2, plus[axis]),
+            remote(line_block(part, 3, 0, chunk), landing(1, 0), base + 3, minus[axis]),
+            remote(line_relay(part, 0, chunk), landing(0, 0), base + 4, plus[axis]),
+            remote(line_relay(part, 1, chunk), landing(1, 1), base + 5, minus[axis]),
+        ]
+
+    def gather(base, axis, slot):
         here = coord[axis]
         left, right = step_of(axis, 3), step_of(axis, 1)
         return [
@@ -153,7 +184,7 @@
 
     fetch_raw, fetch_mom = [], []
     for part in range(PARTS):
-        fetch_raw.append(local(grad_ref.at[layer_of(part, 0)], raw_own(part), part))
+        fetch_raw.append(local(grad_ref.at[layer_of(part, 0)], x_buf.at[part // 2, :, pl.ds(part % 2 * cols, cols)], part))
         fetch_mom.append(local(mom_ref.at[layer_of(part, 0)], mom_own(part), PARTS + part))
     for fetch in fetch_raw + fetch_mom:
         fetch.start()
@@ -163,87 +194,127 @@
         pl.semaphore_signal(barrier, inc=1, device_id=device, device_id_type=MESH)
     pl.semaphore_wait(barrier, 2 * PARTS + 1)
 
-    copies1, copies2, copies3, copies4, copies5, copies6 = [], [], [], [], [], []
-    for part in range(PARTS):
-        def raw_block(j, at, size, part=part):
-            return grad_ref.at[part * SIDE + j, pl.ds(at, size)]
-
-        copies1.append(spread(0, part, part, raw_block, rows, raw_relay, raw_in))
-        launch(copies1[part])
-    for part in range(PARTS):
-        forward(copies1[part])
-
-    for part in range(PARTS):
+    chunks, parts = range(CHUNKS), range(PARTS)
+    copies1 = [[spread(part, chunk) for part in parts] for chunk in chunks]
+    copies2 = [[reduce(part, chunk) for part in parts] for chunk in chunks]
+    copies3, copies4, copies5, copies6 = ([[] for chunk in chunks] for phase in range(4))
+
+    def sum_raw(part, chunk):
+        arrive(copies1[chunk][part])
+        own, into = raw_own(part, chunk), sum_line(part, chunk)
+        first, second, third = (raw_in(part, slot, chunk) for slot in range(3))
+
+        def add(at):
+            total = own[at].astype(jnp.float32) + first[at].astype(jnp.float32)
+            into[at] = (total + second[at].astype(jnp.float32)) + third[at].astype(jnp.float32)
+
+        over_rows(rows, 48, add)
+        launch(copies2[chunk][part])
+
+    def sum_relay(part, chunk):
+        for way, distance in ((0, 1), (1, 3)):
+            copies2[chunk][part][way].wait_recv()
+            relay, own = line_relay(part, way, chunk), line_block(part, distance, way, chunk)
+
+            def add(at, relay=relay, own=own):
+                relay[at] = relay[at] + own[at]
+
+            over_rows(eighth, 24, add)
+            copies2[chunk][part][4 + way].start()
+
+    def sum_line_in(part, chunk):
+        arrive(copies2[chunk][part])
+        axis_c = axes_of(part)[2]
+        into = plane(part, coord[axis_c], chunk)
+        for which in range(2):
+            own = line_block(part, 0, which, chunk)
+
+            def add(at, own=own, which=which):
+                row = pl.ds(pl.multiple_of(which * eighth + at.start, 8), at.size)
+                into[row] = own[at] + (line_in(part, 0, chunk)[row] + line_in(part, 1, chunk)[row])
+
+            over_rows(eighth, 24, add)
+
+        def slot(index, which):
+            return plane(part, index, chunk).at[pl.ds(which * eighth, eighth)]
+
+        copies3[chunk].append(gather(base_of(2, part, chunk), axis_c, slot))
+        launch(copies3[chunk][part])
+
+    def sum_plane(part, chunk):
+        arrive(copies3[chunk][part])
+        axis_b = axes_of(part)[1]
+        layer = layer_of(part, 0)
+        one, two, three, four = (plane(part, slot, chunk) for slot in range(SIDE))
+
+        def add(at):
+            own_at = pl.ds(pl.multiple_of(coord[axis_b] * quarter + at.start, 8), at.size)
+            total = (one[at] + two[at]) + (three[at] + four[at])
+            mom_out[layer, own_at, columns(chunk)] = total * (1.0 / data_size)
+
+        over_rows(quarter, 48, add)
+
+        def slot(index, which):
+            return mom_out.at[layer, pl.ds(pl.multiple_of(index * quarter + which * eighth, 8), eighth), columns(chunk)]
+
+        copies4[chunk].append(gather(base_of(3, part, chunk), axis_b, slot))
+        launch(copies4[chunk][part])
+
+    def spread_mean(part, chunk):
+        arrive(copies4[chunk][part])
+
+        def slot(index, which):
+            return mom_out.at[part * SIDE + index, pl.ds(which * half, half), columns(chunk)]
+
+        copies5[chunk].append(gather(base_of(4, part, chunk), part, slot))
+        for copy in copies5[chunk][part][:2]:
+            copy.start()
+
+    for part in parts:
+        launch(copies1[0][part])
+    for part in parts:
+        for copy in copies1[1][part][:2]:
+            copy.start()
+    for part in parts:
+        forward(copies1[0][part])
+        for copy in copies1[1][part][2:4]:
+            copy.start()
+    for part in parts:
+        forward(copies1[1][part])
+    for part in parts:
         fetch_raw[part].wait()
-        arrive(copies1[part])
-
-        def add_line(at, part=part):
-            total = raw_own(part)[at].astype(jnp.float32) + raw_in(part, 0)[at].astype(jnp.float32)
-            total = total + raw_in(part, 1)[at].astype(jnp.float32)
-            sum_line(part)[at] = total + raw_in(part, 2)[at].astype(jnp.float32)
-
-        over_rows(rows, 16, add_line)
-
-        def quarter_block(j, at, size, part=part):
-            return sum_line(part).at[pl.ds(pl.multiple_of(j * quarter + at, 8), size)]
-
-        copies2.append(spread(1, part, axes_of(part)[1], quarter_block, quarter, line_relay, line_in))
-        launch(copies2[part])
-    for part in range(PARTS):
-        forward(copies2[part])
-
-    for part in range(PARTS):
-        arrive(copies2[part])
-        axis_b, axis_c = axes_of(part)[1:]
-
-        def add_plane(at, part=part, axis_b=axis_b, axis_c=axis_c):
-            own_at = pl.ds(pl.multiple_of(coord[axis_b] * quarter + at.start, 8), at.size)
-            plane(part, coord[axis_c])[at] = (sum_line(part)[own_at] + line_in(part, 0)[at]) + (
-                line_in(part, 1)[at] + line_in(part, 2)[at])
-
-        over_rows(quarter, 16, add_plane)
-
-        def plane_slot(slot, which, part=part):
-            return plane(part, slot).at[pl.ds(which * eighth, eighth)]
-
-        copies3.append(gather(2, part, axis_c, plane_slot))
-        launch(copies3[part])
-    for part in range(PARTS):
-        forward(copies3[part])
-
-    for part in range(PARTS):
-        arrive(copies3[part])
-        axis_b = axes_of(part)[1]
-
-        def add_cube(at, part=part, axis_b=axis_b):
-            own_at = pl.ds(pl.multiple_of(coord[axis_b] * quarter + at.start, 8), at.size)
-            total = (plane(part, 0)[at] + plane(part, 1)[at]) + (plane(part, 2)[at] + plane(part, 3)[at])
-            mom_out[layer_of(part, 0), own_at] = total * (1.0 / data_size)
-
-        over_rows(quarter, 16, add_cube)
-
-        def mean_slot(slot, which, part=part):
-            return mom_out.at[layer_of(part, 0), pl.ds(pl.multiple_of(slot * quarter + which * eighth, 8), eighth)]
-
-        copies4.append(gather(3, part, axis_b, mean_slot))
-        launch(copies4[part])
-    for part in range(PARTS):
-        forward(copies4[part])
-    for part in range(PARTS):
-        sent(copies1[part])
-        sent(copies2[part])
-        sent(copies3[part])
-
-    for part in range(PARTS):
-        arrive(copies4[part])
-
-        def mean_block(slot, which, part=part):
-            return mom_out.at[part * SIDE + slot, pl.ds(which * half, half)]
-
-        copies5.append(gather(4, part, part, mean_block))
-        launch(copies5[part])
-
-    swap_base = PHASES * PARTS * KINDS
+        sum_raw(part, 0)
+    for part in parts:
+        sum_raw(part, 1)
+    for chunk in chunks:
+        for part in parts:
+            sum_relay(part, chunk)
+    for chunk in chunks:
+        for part in parts:
+            sum_line_in(part, chunk)
+    for chunk in chunks:
+        for part in parts:
+            forward(copies3[chunk][part])
+    for chunk in chunks:
+        for part in parts:
+            sum_plane(part, chunk)
+    for chunk in chunks:
+        for part in parts:
+            forward(copies4[chunk][part])
+    for chunk in chunks:
+        for part in parts:
+            sent(copies1[chunk][part])
+            sent(copies2[chunk][part])
+            sent(copies3[chunk][part])
+    for chunk in chunks:
+        for part in parts:
+            spread_mean(part, chunk)
+    for chunk in chunks:
+        for part in parts:
+            for copy in copies5[chunk][part][2:4]:
+                copy.start()
+
+    swap_base = base_of(PHASES, 0)
     for part in range(PARTS):
         fetch_mom[part].wait()
 
@@ -306,15 +377,16 @@
         def slot(index, which):
             return ortho_all.at[part * SIDE + index, pl.ds(which * half, half)]
 
-        copies6.append(gather(5, part, part, slot))
-        launch(copies6[part])
+        copies6[0].append(gather(base_of(5, part), part, slot))
+        launch(copies6[0][part])
 
     give_first.wait_recv()
     orthogonalise(tp_idx, 0)
     swap_x = remote(x_buf.at[final, :, pl.ds(cols, cols)], ortho_all.at[first_layer], swap_base + 2, partner)
     swap_x.start()
-    for part in range(PARTS):
-        forward(copies5[part])
+    for chunk in chunks:
+        for part in parts:
+            forward(copies5[chunk][part])
     keep_half(first_layer)
     swap_x.wait()
     ortho_gather(0)
@@ -347,18 +419,20 @@
     fetch_turn[0].start()
     fetch_turn[1].start()
     for index, (part, distance) in enumerate(turns):
-        if distance == 0:
-            sent(copies4[part])
-            sent(copies5[part][:4])
-        elif distance == 3:
-            copies5[part][2].wait_recv()
-            copies5[part][4].wait_send()
-        elif distance == 1:
-            copies5[part][3].wait_recv()
-            copies5[part][5].wait_send()
-        else:
-            copies5[part][4].wait_recv()
-            copies5[part][5].wait_recv()
+        for chunk in chunks:
+            copies = copies5[chunk][part]
+            if distance == 0:
+                sent(copies4[chunk][part])
+                sent(copies[:4])
+            elif distance == 3:
+                copies[2].wait_recv()
+                copies[4].wait_send()
+            elif distance == 1:
+                copies[3].wait_recv()
+                copies[5].wait_send()
+            else:
+                copies[4].wait_recv()
+                copies[5].wait_recv()
         fetch_turn[index].wait()
         layer = layer_of(part, distance)
 
@@ -370,17 +444,17 @@
             fetch_turn[index + 2].start()
 
     for part in range(PARTS):
-        forward(copies6[part])
+        forward(copies6[0][part])
     for fetch in fetch_weight:
         fetch.wait()
     for part, distance in turns:
         if distance == 3:
-            copies6[part][2].wait_recv()
+            copies6[0][part][2].wait_recv()
         elif distance == 1:
-            copies6[part][3].wait_recv()
+            copies6[0][part][3].wait_recv()
         elif distance == 2:
-            copies6[part][4].wait_recv()
-            copies6[part][5].wait_recv()
+            copies6[0][part][4].wait_recv()
+            copies6[0][part][5].wait_recv()
         layer = layer_of(part, distance)
 
         def descend(at, layer=layer):
@@ -390,7 +464,7 @@
 
         over_rows(rows, 16, descend)
     for part in range(PARTS):
-        sent(copies6[part])
+        sent(copies6[0][part])
 
 
 def flush(held, mom_ref, weight_ref, sem):
@@ -413,7 +487,7 @@
 
     def per_device(weight, momentum, grad):
         layers, rows, cols = weight.shape
-        copies = PHASES * PARTS * KINDS + SWAPS
+        copies = PHASES * CHUNKS * PARTS * KINDS + SWAPS
         rms_scale = 0.2 * math.sqrt(max(rows, cols * tp_size))
         bf16, f32 = jnp.bfloat16, jnp.float32
         in_hbm = pl.BlockSpec(memory_space=pltpu.HBM)

time: 204 us -> 196 us (0.961)
  Pallas kernels: 202 us -> 195 us
    pallas_call x1, Pallas kernels: 188 us -> 181 us  [per_device(): pl.pallas_call(functools.partial(kernel, rows, cols, data_size, rms_scale...]
where the time goes in v4:
time: 196 us; the launch traced here: 195 us
  Pallas kernels  195 us (99%)
    pallas_call x1, Pallas kernels, per_device(): pl.pallas_call(functools.partial(kernel, rows, cols, data_size, rms_scale...  181 us
    pallas_call x1, Pallas kernels, per_device(): pl.pallas_call(flush, out_shape=(jax.ShapeDtypeStruct((layers, rows, cols...  13.8 us

profile of v4, /device:TPU:1, one launch (start us, length us, event | category | flops | bytes accessed | tf_op | source)
XLA Modules:
  0.0 195.3 jit_solution(12796136442055060760)
XLA Ops:
  0.6 180.9 %shard_map.50.held = f32[24,576,768]{2,1,0:T(8,128)S(1)} custom-call(bf16[12,576,768]{2,1,0:T(8,128)(2,1)} %bitcast.1, f32[12,576,768]{2,1,0:T(8,128)} %mom_ref.1, f32[12,576,768]{2,1,0:T(8,128)} %weight_ref.1), custom_call_target="tpu_custom_call" | custom-call | tf_op jit(solution)/shard_map/pallas_call | solution.py:495
  181.5 13.8 %shard_map.51 = (f32[12,576,768]{2,1,0:T(8,128)}, f32[12,576,768]{2,1,0:T(8,128)}) custom-call(f32[24,576,768]{2,1,0:T(8,128)S(1)} %shard_map.50.held), custom_call_target="tpu_custom_call" | custom-call | tf_op jit(solution)/shard_map/pallas_call | solution.py:512

commit v5 on v4

--- a/solution.py
+++ b/solution.py
@@ -20,8 +20,8 @@
 SIDE = 4
 PARTS = 3
 STRIDES = (1, 4, 16)
+JOINED = 4
 KINDS = 6
-PHASES = 6
 CHUNKS = 2
 SWAPS = 4
 VMEM_KERNEL = 22 * 1024 * 1024
@@ -35,6 +35,22 @@
 
 def dot_nt(lhs, rhs):
     return lax.dot_general(lhs, rhs, (((1,), (1,)), ((), ())), preferred_element_type=jnp.float32)
+
+
+def over_rows(count, chunk, body):
+    def run(index, carry):
+        body(pl.ds(pl.multiple_of(index * chunk, chunk), chunk))
+        return carry
+    lax.fori_loop(0, count // chunk, run, 0)
+
+
+def descend(weight_out, ortho_all, rms_scale, layer):
+    def add(at):
+        weight = weight_out[layer, at]
+        ortho = ortho_all[layer, at].astype(jnp.float32)
+        weight_out[layer, at] = weight - LEARN_RATE * (rms_scale * ortho + WEIGHT_DECAY * weight)
+
+    over_rows(weight_out.shape[1], 48, add)
 
 
 def kernel(rows, cols, data_size, rms_scale, grad_ref, mom_ref, weight_ref, held, ortho_all, x_buf, gram_buf, poly_buf,
@@ -97,18 +113,25 @@
     def axes_of(part):
         return part, (part + 1) % PARTS, (part + 2) % PARTS
 
-    def remote(src, dst, index, device):
-        return pltpu.make_async_remote_copy(src_ref=src, dst_ref=dst, send_sem=send_sem.at[index],
-                                            recv_sem=recv_sem.at[index], device_id=device, device_id_type=MESH)
-
-    def base_of(phase, part, chunk=0):
-        return ((phase * CHUNKS + chunk) * PARTS + part) * KINDS
+    def remote(src, dst, send, receive, device):
+        return pltpu.make_async_remote_copy(src_ref=src, dst_ref=dst, send_sem=send_sem.at[send],
+                                            recv_sem=recv_sem.at[receive], device_id=device, device_id_type=MESH)
+
+    def numbers(phase, part, chunk, kind):
+        group = chunk * PARTS + part
+        send = (phase % 2 * CHUNKS * PARTS + group) * KINDS + kind
+        if phase < JOINED:
+            return send, (phase * CHUNKS * PARTS + group) * 3 + min(kind, 2)
+        return send, (JOINED * 3 + (phase - JOINED) * KINDS) * CHUNKS * PARTS + group * KINDS + kind
+
+    def arrive(phase, part, chunk, landed):
+        remote(landed, landed, *numbers(phase, part, chunk, 2), partner).wait_recv()
 
     def local(src, dst, index):
         return pltpu.make_async_copy(src, dst, local_sem.at[index])
 
     def spread(part, chunk):
-        base = base_of(0, part, chunk)
+        at_of = functools.partial(numbers, 0, part, chunk)
         far, right, left = layer_of(part, 2), layer_of(part, 1), layer_of(part, 3)
 
         def block(layer, at, size):
@@ -118,12 +141,12 @@
             return raw_in(part, slot, chunk).at[pl.ds(at, size)]
 
         return [
-            remote(block(far, 0, half), raw_relay(part, 0, chunk), base + 0, plus[part]),
-            remote(block(far, half, half), raw_relay(part, 1, chunk), base + 1, minus[part]),
-            remote(block(right, 0, rows), landing(0, 0, rows), base + 2, plus[part]),
-            remote(block(left, 0, rows), landing(1, 0, rows), base + 3, minus[part]),
-            remote(raw_relay(part, 0, chunk), landing(2, 0, half), base + 4, plus[part]),
-            remote(raw_relay(part, 1, chunk), landing(2, half, half), base + 5, minus[part]),
+            remote(block(far, 0, half), raw_relay(part, 0, chunk), *at_of(0), plus[part]),
+            remote(block(far, half, half), raw_relay(part, 1, chunk), *at_of(1), minus[part]),
+            remote(block(right, 0, rows), landing(0, 0, rows), *at_of(2), plus[part]),
+            remote(block(left, 0, rows), landing(1, 0, rows), *at_of(3), minus[part]),
+            remote(raw_relay(part, 0, chunk), landing(2, 0, half), *at_of(4), plus[part]),
+            remote(raw_relay(part, 1, chunk), landing(2, half, half), *at_of(5), minus[part]),
         ]
 
     def line_block(part, distance, which, chunk):
@@ -131,31 +154,32 @@
         return sum_line(part, chunk).at[pl.ds(pl.multiple_of(at, 8), eighth)]
 
     def reduce(part, chunk):
-        base = base_of(1, part, chunk)
+        at_of = functools.partial(numbers, 1, part, chunk)
         axis = axes_of(part)[1]
 
         def landing(slot, which):
             return line_in(part, slot, chunk).at[pl.ds(which * eighth, eighth)]
 
         return [
-            remote(line_block(part, 2, 0, chunk), line_relay(part, 0, chunk), base + 0, plus[axis]),
-            remote(line_block(part, 2, 1, chunk), line_relay(part, 1, chunk), base + 1, minus[axis]),
-            remote(line_block(part, 1, 1, chunk), landing(0, 1), base + 2, plus[axis]),
-            remote(line_block(part, 3, 0, chunk), landing(1, 0), base + 3, minus[axis]),
-            remote(line_relay(part, 0, chunk), landing(0, 0), base + 4, plus[axis]),
-            remote(line_relay(part, 1, chunk), landing(1, 1), base + 5, minus[axis]),
+            remote(line_block(part, 2, 0, chunk), line_relay(part, 0, chunk), *at_of(0), plus[axis]),
+            remote(line_block(part, 2, 1, chunk), line_relay(part, 1, chunk), *at_of(1), minus[axis]),
+            remote(line_block(part, 1, 1, chunk), landing(0, 1), *at_of(2), plus[axis]),
+            remote(line_block(part, 3, 0, chunk), landing(1, 0), *at_of(3), minus[axis]),
+            remote(line_relay(part, 0, chunk), landing(0, 0), *at_of(4), plus[axis]),
+            remote(line_relay(part, 1, chunk), landing(1, 1), *at_of(5), minus[axis]),
         ]
 
-    def gather(base, axis, slot):
+    def gather(phase, part, chunk, axis, slot):
+        at_of = functools.partial(numbers, phase, part, chunk)
         here = coord[axis]
         left, right = step_of(axis, 3), step_of(axis, 1)
         return [
-            remote(slot(here, 0), slot(here, 0), base + 0, plus[axis]),
-            remote(slot(here, 1), slot(here, 1), base + 1, minus[axis]),
-            remote(slot(here, 1), slot(here, 1), base + 2, plus[axis]),
-            remote(slot(here, 0), slot(here, 0), base + 3, minus[axis]),
-            remote(slot(left, 0), slot(left, 0), base + 4, plus[axis]),
-            remote(slot(right, 1), slot(right, 1), base + 5, minus[axis]),
+            remote(slot(here, 0), slot(here, 0), *at_of(0), plus[axis]),
+            remote(slot(here, 1), slot(here, 1), *at_of(1), minus[axis]),
+            remote(slot(here, 1), slot(here, 1), *at_of(2), plus[axis]),
+            remote(slot(here, 0), slot(here, 0), *at_of(3), minus[axis]),
+            remote(slot(left, 0), slot(left, 0), *at_of(4), plus[axis]),
+            remote(slot(right, 1), slot(right, 1), *at_of(5), minus[axis]),
         ]
 
     def launch(copies):
@@ -168,19 +192,9 @@
         copies[1].wait_recv()
         copies[5].start()
 
-    def arrive(copies):
-        for copy in copies[2:]:
-            copy.wait_recv()
-
     def sent(copies):
         for copy in copies:
             copy.wait_send()
-
-    def over_rows(count, chunk, body):
-        def run(index, carry):
-            body(pl.ds(pl.multiple_of(index * chunk, chunk), chunk))
-            return carry
-        lax.fori_loop(0, count // chunk, run, 0)
 
     fetch_raw, fetch_mom = [], []
     for part in range(PARTS):
@@ -200,7 +214,7 @@
     copies3, copies4, copies5, copies6 = ([[] for chunk in chunks] for phase in range(4))
 
     def sum_raw(part, chunk):
-        arrive(copies1[chunk][part])
+        arrive(0, part, chunk, ortho_all.at[pl.ds(part * 3, 3), :, columns(chunk)])
         own, into = raw_own(part, chunk), sum_line(part, chunk)
         first, second, third = (raw_in(part, slot, chunk) for slot in range(3))
 
@@ -223,7 +237,7 @@
             copies2[chunk][part][4 + way].start()
 
     def sum_line_in(part, chunk):
-        arrive(copies2[chunk][part])
+        arrive(1, part, chunk, weight_out.at[PARTS + part, pl.ds(0, 2 * quarter), columns(chunk)])
         axis_c = axes_of(part)[2]
         into = plane(part, coord[axis_c], chunk)
         for which in range(2):
@@ -238,11 +252,11 @@
         def slot(index, which):
             return plane(part, index, chunk).at[pl.ds(which * eighth, eighth)]
 
-        copies3[chunk].append(gather(base_of(2, part, chunk), axis_c, slot))
+        copies3[chunk].append(gather(2, part, chunk, axis_c, slot))
         launch(copies3[chunk][part])
 
     def sum_plane(part, chunk):
-        arrive(copies3[chunk][part])
+        arrive(2, part, chunk, weight_out.at[2 * PARTS + part, pl.ds(0, 2 * quarter), columns(chunk)])
         axis_b = axes_of(part)[1]
         layer = layer_of(part, 0)
         one, two, three, four = (plane(part, slot, chunk) for slot in range(SIDE))
@@ -257,16 +271,16 @@
         def slot(index, which):
             return mom_out.at[layer, pl.ds(pl.multiple_of(index * quarter + which * eighth, 8), eighth), columns(chunk)]
 
-        copies4[chunk].append(gather(base_of(3, part, chunk), axis_b, slot))
+        copies4[chunk].append(gather(3, part, chunk, axis_b, slot))
         launch(copies4[chunk][part])
 
     def spread_mean(part, chunk):
-        arrive(copies4[chunk][part])
+        arrive(3, part, chunk, mom_out.at[layer_of(part, 0), pl.ds(0, 2 * quarter), columns(chunk)])
 
         def slot(index, which):
             return mom_out.at[part * SIDE + index, pl.ds(which * half, half), columns(chunk)]
 
-        copies5[chunk].append(gather(base_of(4, part, chunk), part, slot))
+        copies5[chunk].append(gather(4, part, chunk, part, slot))
         for copy in copies5[chunk][part][:2]:
             copy.start()
 
@@ -291,20 +305,24 @@
             sum_relay(part, chunk)
     for chunk in chunks:
         for part in parts:
+            sent(copies1[chunk][part])
+    for chunk in chunks:
+        for part in parts:
             sum_line_in(part, chunk)
     for chunk in chunks:
         for part in parts:
             forward(copies3[chunk][part])
     for chunk in chunks:
         for part in parts:
+            sent(copies2[chunk][part])
+    for chunk in chunks:
+        for part in parts:
             sum_plane(part, chunk)
     for chunk in chunks:
         for part in parts:
             forward(copies4[chunk][part])
     for chunk in chunks:
         for part in parts:
-            sent(copies1[chunk][part])
-            sent(copies2[chunk][part])
             sent(copies3[chunk][part])
     for chunk in chunks:
         for part in parts:
@@ -314,7 +332,7 @@
             for copy in copies5[chunk][part][2:4]:
                 copy.start()
 
-    swap_base = base_of(PHASES, 0)
+    swap_send, swap_receive = 2 * CHUNKS * PARTS * KINDS, (JOINED * 3 + KINDS) * CHUNKS * PARTS + KINDS * PARTS
     for part in range(PARTS):
         fetch_mom[part].wait()
 
@@ -323,16 +341,16 @@
             nest(part)[at] = mean + MOMENTUM * (MOMENTUM * mom_own(part)[at] + mean)
 
         over_rows(rows, 16, nesterov)
-    give_first = remote(weight_out.at[1 - tp_idx], nest_in.at[0], swap_base, partner)
+    give_first = remote(weight_out.at[1 - tp_idx], nest_in.at[0], swap_send + 0, swap_receive + 0, partner)
     give_first.start()
-    give_second = remote(nest(2), nest_in.at[1], swap_base + 1, partner)
+    give_second = remote(nest(2), nest_in.at[1], swap_send + 1, swap_receive + 1, partner)
 
     @pl.when(tp_idx == 1)
     def _():
         give_second.start()
 
     weight_base = 2 * PARTS
-    fetch_weight = [local(weight_ref.at[layer], weight_out.at[layer], weight_base + layer) for layer in range(layers)]
+    fetch_weight = [local(weight_ref.at[layer], weight_out.at[layer], weight_base) for layer in range(layers)]
     for fetch in fetch_weight[PARTS:]:
         fetch.start()
 
@@ -377,22 +395,25 @@
         def slot(index, which):
             return ortho_all.at[part * SIDE + index, pl.ds(which * half, half)]
 
-        copies6[0].append(gather(base_of(5, part), part, slot))
+        copies6[0].append(gather(5, part, 0, part, slot))
         launch(copies6[0][part])
 
     give_first.wait_recv()
     orthogonalise(tp_idx, 0)
-    swap_x = remote(x_buf.at[final, :, pl.ds(cols, cols)], ortho_all.at[first_layer], swap_base + 2, partner)
+    swap_x = remote(x_buf.at[final, :, pl.ds(cols, cols)], ortho_all.at[first_layer], swap_send + 2, swap_receive + 2, partner)
     swap_x.start()
     for chunk in chunks:
         for part in parts:
             forward(copies5[chunk][part])
     keep_half(first_layer)
     swap_x.wait()
+    for chunk in chunks:
+        for part in parts:
+            sent(copies4[chunk][part])
     ortho_gather(0)
     ortho_gather(1)
 
-    give_x = remote(x_buf.at[final, :, pl.ds(cols, cols)], ortho_all.at[layer_of(2, 0)], swap_base + 3, partner)
+    give_x = remote(x_buf.at[final, :, pl.ds(cols, cols)], ortho_all.at[layer_of(2, 0)], swap_send + 3, swap_receive + 3, partner)
 
     @pl.when(tp_idx == 0)
     def _():
@@ -412,9 +433,9 @@
     for fetch in fetch_weight[:PARTS]:
         fetch.start()
 
-    stream_base = weight_base + layers
+    stream_base = weight_base + 1
     turns = [(part, distance) for distance in ORDER for part in range(PARTS)]
-    fetch_turn = [local(mom_ref.at[layer_of(*turn)], nest_in.at[index % 2], stream_base + index)
+    fetch_turn = [local(mom_ref.at[layer_of(*turn)], nest_in.at[index % 2], stream_base + index % 2)
                   for index, turn in enumerate(turns)]
     fetch_turn[0].start()
     fetch_turn[1].start()
@@ -422,7 +443,6 @@
         for chunk in chunks:
             copies = copies5[chunk][part]
             if distance == 0:
-                sent(copies4[chunk][part])
                 sent(copies[:4])
             elif distance == 3:
                 copies[2].wait_recv()
@@ -445,8 +465,7 @@
 
     for part in range(PARTS):
         forward(copies6[0][part])
-    for fetch in fetch_weight:
-        fetch.wait()
+    local(weight_ref, weight_out, weight_base).wait()
     for part, distance in turns:
         if distance == 3:
             copies6[0][part][2].wait_recv()
@@ -455,28 +474,20 @@
         elif distance == 2:
             copies6[0][part][4].wait_recv()
             copies6[0][part][5].wait_recv()
-        layer = layer_of(part, distance)
-
-        def descend(at, layer=layer):
-            weight = weight_out[layer, at]
-            ortho = ortho_all[layer, at].astype(jnp.float32)
-            weight_out[layer, at] = weight - LEARN_RATE * (rms_scale * ortho + WEIGHT_DECAY * weight)
-
-        over_rows(rows, 16, descend)
-    for part in range(PARTS):
+        descend(weight_out, ortho_all, rms_scale, layer_of(part, distance))
+    for part in parts:
         sent(copies6[0][part])
 
 
 def flush(held, mom_ref, weight_ref, sem):
     layers = mom_ref.shape[0]
-    copies = []
+    mom_out = held.at[pl.ds(0, layers)]
+    weight_out = held.at[pl.ds(layers, layers)]
     for layer in range(layers):
-        copies.append(pltpu.make_async_copy(held.at[layer], mom_ref.at[layer], sem.at[layer]))
-        copies.append(pltpu.make_async_copy(held.at[layers + layer], weight_ref.at[layer], sem.at[layers + layer]))
-    for copy in copies:
-        copy.start()
-    for copy in copies:
-        copy.wait()
+        pltpu.make_async_copy(mom_out.at[layer], mom_ref.at[layer], sem.at[0]).start()
+        pltpu.make_async_copy(weight_out.at[layer], weight_ref.at[layer], sem.at[1]).start()
+    pltpu.make_async_copy(mom_out, mom_ref, sem.at[0]).wait()
+    pltpu.make_async_copy(weight_out, weight_ref, sem.at[1]).wait()
 
 
 def solution(mesh):
@@ -487,7 +498,8 @@
 
     def per_device(weight, momentum, grad):
         layers, rows, cols = weight.shape
-        copies = PHASES * CHUNKS * PARTS * KINDS + SWAPS
+        sends = 2 * CHUNKS * PARTS * KINDS + SWAPS
+        receives = (JOINED * 3 + KINDS) * CHUNKS * PARTS + KINDS * PARTS + SWAPS
         rms_scale = 0.2 * math.sqrt(max(rows, cols * tp_size))
         bf16, f32 = jnp.bfloat16, jnp.float32
         in_hbm = pl.BlockSpec(memory_space=pltpu.HBM)
@@ -503,9 +515,9 @@
                 pltpu.VMEM((rows, rows), bf16),
                 pltpu.VMEM((rows, rows), bf16),
                 pltpu.VMEM((2, rows, cols), f32),
-                pltpu.SemaphoreType.DMA((copies,)),
-                pltpu.SemaphoreType.DMA((copies,)),
-                pltpu.SemaphoreType.DMA((2 * PARTS + 2 * layers,)),
+                pltpu.SemaphoreType.DMA((sends,)),
+                pltpu.SemaphoreType.DMA((receives,)),
+                pltpu.SemaphoreType.DMA((2 * PARTS + 3,)),
             ],
             compiler_params=pltpu.CompilerParams(collective_id=0, has_side_effects=True, vmem_limit_bytes=VMEM_KERNEL),
         )(grad.reshape(layers, rows, cols), momentum, weight)
@@ -514,7 +526,7 @@
             out_shape=(jax.ShapeDtypeStruct((layers, rows, cols), f32),) * 2,
             in_specs=[in_vmem],
             out_specs=(in_hbm,) * 2,
-            scratch_shapes=[pltpu.SemaphoreType.DMA((2 * layers,))],
+            scratch_shapes=[pltpu.SemaphoreType.DMA((2,))],
             compiler_params=pltpu.CompilerParams(vmem_limit_bytes=VMEM_FLUSH),
         )(held)
         return new_weight, new_mom

time: 196 us -> 193 us (0.985)
  Pallas kernels: 195 us -> 192 us
    pallas_call x1, Pallas kernels: 181 us -> 178 us  [per_device(): pl.pallas_call(functools.partial(kernel, rows, cols, data_size, rms_scale...]
where the time goes in v5:
time: 193 us
  Pallas kernels  192 us (99%)
    pallas_call x1, Pallas kernels, per_device(): pl.pallas_call(functools.partial(kernel, rows, cols, data_size, rms_scale...  178 us
    pallas_call x1, Pallas kernels, per_device(): pl.pallas_call(flush, out_shape=(jax.ShapeDtypeStruct((layers, rows, cols...  13.6 us

profile of v5, /device:TPU:1, one launch (start us, length us, event | category | flops | bytes accessed | tf_op | source)
XLA Modules:
  0.0 192.7 jit_solution(4668754218858792885)
XLA Ops:
  0.6 178.5 %shard_map.50.held = f32[24,576,768]{2,1,0:T(8,128)S(1)} custom-call(bf16[12,576,768]{2,1,0:T(8,128)(2,1)} %bitcast.1, f32[12,576,768]{2,1,0:T(8,128)} %mom_ref.1, f32[12,576,768]{2,1,0:T(8,128)} %weight_ref.1), custom_call_target="tpu_custom_call" | custom-call | tf_op jit(solution)/shard_map/pallas_call | solution.py:507
  179.1 13.6 %shard_map.51 = (f32[12,576,768]{2,1,0:T(8,128)}, f32[12,576,768]{2,1,0:T(8,128)}) custom-call(f32[24,576,768]{2,1,0:T(8,128)S(1)} %shard_map.50.held), custom_call_target="tpu_custom_call" | custom-call | tf_op jit(solution)/shard_map/pallas_call | solution.py:524

commit v6 on v5

--- a/solution.py
+++ b/solution.py
@@ -20,9 +20,12 @@
 SIDE = 4
 PARTS = 3
 STRIDES = (1, 4, 16)
-JOINED = 4
+JOINED = 5
 KINDS = 6
-CHUNKS = 2
+CHUNKS = 3
+GROUPS = (2, 1)
+LANES = 128
+SPLIT = 40
 SWAPS = 4
 VMEM_KERNEL = 22 * 1024 * 1024
 VMEM_FLUSH = 1024 * 1024
@@ -88,8 +91,28 @@
     def line_relay(part, way, chunk):
         return weight_out.at[PARTS + part, pl.ds(2 * quarter + way * eighth, eighth), columns(chunk)]
 
-    def plane(part, slot, chunk):
-        return weight_out.at[2 * PARTS + part, pl.ds(pl.multiple_of(slot * quarter, 8), quarter), columns(chunk)]
+    block_rows = eighth
+
+    def block_at(index, which, row, chunk):
+        at = row + lax.div(index, 2) * block_rows + which * SPLIT
+        size = block_rows - SPLIT if which else SPLIT
+        lane = chunk * width + lax.rem(index, 2) * LANES
+        return pl.ds(pl.multiple_of(at, 8), size), pl.ds(pl.multiple_of(lane, LANES), LANES)
+
+    def plane(part, chunk):
+        return weight_out.at[2 * PARTS + part, pl.ds(0, quarter), columns(chunk)]
+
+    def plane_block(part, index, which, chunk):
+        return weight_out.at[2 * PARTS + part, *block_at(index, which, 0, chunk)]
+
+    def plane_in(part, slot, which, chunk):
+        size = block_rows - SPLIT if which else SPLIT
+        return weight_out.at[2 * PARTS + part, pl.ds(quarter + slot * block_rows + which * SPLIT, size),
+                             pl.ds(chunk * width, LANES)]
+
+    def plane_relay(part, way, chunk):
+        size = block_rows - SPLIT if way else SPLIT
+        return weight_out.at[2 * PARTS + part, pl.ds(quarter + way * SPLIT, size), pl.ds(chunk * width + LANES, LANES)]
 
     def mom_own(part):
         return weight_out.at[3 * PARTS + part]
@@ -119,13 +142,30 @@
 
     def numbers(phase, part, chunk, kind):
         group = chunk * PARTS + part
-        send = (phase % 2 * CHUNKS * PARTS + group) * KINDS + kind
+        send = phase % 2 * CHUNKS * PARTS + group
         if phase < JOINED:
             return send, (phase * CHUNKS * PARTS + group) * 3 + min(kind, 2)
-        return send, (JOINED * 3 + (phase - JOINED) * KINDS) * CHUNKS * PARTS + group * KINDS + kind
+        later = JOINED * 3 * CHUNKS * PARTS + (phase - JOINED) * len(GROUPS) * PARTS * KINDS
+        return send, later + group * KINDS + kind
 
     def arrive(phase, part, chunk, landed):
         remote(landed, landed, *numbers(phase, part, chunk, 2), partner).wait_recv()
+
+    def sent(phase, part, chunk=0):
+        if phase == 0:
+            left = ortho_all.at[pl.ds(0, SIDE), :, columns(chunk)]
+        elif phase in (1, 4):
+            left = weight_out.at[0, pl.ds(0, 3 * quarter), columns(chunk)]
+        elif phase in (2, 3):
+            left = weight_out.at[0, pl.ds(0, 3 * block_rows), pl.ds(0, LANES)]
+        elif phase == 5:
+            left = mom_out.at[pl.ds(0, 3), :, group_columns(chunk)]
+        else:
+            left = ortho_all.at[pl.ds(0, 3)]
+        remote(left, left, *numbers(phase, part, chunk, 2), partner).wait_send()
+
+    def group_columns(group):
+        return pl.ds(sum(GROUPS[:group]) * width, GROUPS[group] * width)
 
     def local(src, dst, index):
         return pltpu.make_async_copy(src, dst, local_sem.at[index])
@@ -153,21 +193,41 @@
         at = step_of(axes_of(part)[1], distance) * quarter + which * eighth
         return sum_line(part, chunk).at[pl.ds(pl.multiple_of(at, 8), eighth)]
 
-    def reduce(part, chunk):
-        at_of = functools.partial(numbers, 1, part, chunk)
-        axis = axes_of(part)[1]
-
+    def reduce(phase, part, chunk, axis, block, relay, landing):
+        at_of = functools.partial(numbers, phase, part, chunk)
+        return [
+            remote(block(2, 0), relay(0), *at_of(0), plus[axis]),
+            remote(block(2, 1), relay(1), *at_of(1), minus[axis]),
+            remote(block(1, 1), landing(0, 1), *at_of(2), plus[axis]),
+            remote(block(3, 0), landing(1, 0), *at_of(3), minus[axis]),
+            remote(relay(0), landing(0, 0), *at_of(4), plus[axis]),
+            remote(relay(1), landing(1, 1), *at_of(5), minus[axis]),
+        ]
+
+    def relay_sums(copies, block, relay):
+        for way, distance in ((0, 1), (1, 3)):
+            copies[way].wait_recv()
+            into, own = relay(way), block(distance, way)
+
+            def add(at, into=into, own=own):
+                into[at] = into[at] + own[at]
+
+            over_rows(into.shape[0], 8, add)
+            copies[4 + way].start()
+
+    def reduce_rows(part, chunk):
         def landing(slot, which):
             return line_in(part, slot, chunk).at[pl.ds(which * eighth, eighth)]
 
-        return [
-            remote(line_block(part, 2, 0, chunk), line_relay(part, 0, chunk), *at_of(0), plus[axis]),
-            remote(line_block(part, 2, 1, chunk), line_relay(part, 1, chunk), *at_of(1), minus[axis]),
-            remote(line_block(part, 1, 1, chunk), landing(0, 1), *at_of(2), plus[axis]),
-            remote(line_block(part, 3, 0, chunk), landing(1, 0), *at_of(3), minus[axis]),
-            remote(line_relay(part, 0, chunk), landing(0, 0), *at_of(4), plus[axis]),
-            remote(line_relay(part, 1, chunk), landing(1, 1), *at_of(5), minus[axis]),
-        ]
+        return reduce(1, part, chunk, axes_of(part)[1], lambda distance, which: line_block(part, distance, which, chunk),
+                      lambda way: line_relay(part, way, chunk), landing)
+
+    def third_block(part, distance, which, chunk):
+        return plane_block(part, step_of(axes_of(part)[2], distance), which, chunk)
+
+    def reduce_blocks(part, chunk):
+        return reduce(2, part, chunk, axes_of(part)[2], lambda distance, which: third_block(part, distance, which, chunk),
+                      lambda way: plane_relay(part, way, chunk), lambda slot, which: plane_in(part, slot, which, chunk))
 
     def gather(phase, part, chunk, axis, slot):
         at_of = functools.partial(numbers, phase, part, chunk)
@@ -192,10 +252,6 @@
         copies[1].wait_recv()
         copies[5].start()
 
-    def sent(copies):
-        for copy in copies:
-            copy.wait_send()
-
     fetch_raw, fetch_mom = [], []
     for part in range(PARTS):
         fetch_raw.append(local(grad_ref.at[layer_of(part, 0)], x_buf.at[part // 2, :, pl.ds(part % 2 * cols, cols)], part))
@@ -210,8 +266,9 @@
 
     chunks, parts = range(CHUNKS), range(PARTS)
     copies1 = [[spread(part, chunk) for part in parts] for chunk in chunks]
-    copies2 = [[reduce(part, chunk) for part in parts] for chunk in chunks]
-    copies3, copies4, copies5, copies6 = ([[] for chunk in chunks] for phase in range(4))
+    copies2 = [[reduce_rows(part, chunk) for part in parts] for chunk in chunks]
+    copies3 = [[reduce_blocks(part, chunk) for part in parts] for chunk in chunks]
+    copies4, copies5, copies6, copies7 = ({}, {}, {}, {})
 
     def sum_raw(part, chunk):
         arrive(0, part, chunk, ortho_all.at[pl.ds(part * 3, 3), :, columns(chunk)])
@@ -225,21 +282,13 @@
         over_rows(rows, 48, add)
         launch(copies2[chunk][part])
 
-    def sum_relay(part, chunk):
-        for way, distance in ((0, 1), (1, 3)):
-            copies2[chunk][part][way].wait_recv()
-            relay, own = line_relay(part, way, chunk), line_block(part, distance, way, chunk)
-
-            def add(at, relay=relay, own=own):
-                relay[at] = relay[at] + own[at]
-
-            over_rows(eighth, 24, add)
-            copies2[chunk][part][4 + way].start()
-
-    def sum_line_in(part, chunk):
+    def relay_rows(part, chunk):
+        relay_sums(copies2[chunk][part], lambda distance, way: line_block(part, distance, way, chunk),
+                   lambda way: line_relay(part, way, chunk))
+
+    def sum_rows(part, chunk):
         arrive(1, part, chunk, weight_out.at[PARTS + part, pl.ds(0, 2 * quarter), columns(chunk)])
-        axis_c = axes_of(part)[2]
-        into = plane(part, coord[axis_c], chunk)
+        into = plane(part, chunk)
         for which in range(2):
             own = line_block(part, 0, which, chunk)
 
@@ -248,91 +297,105 @@
                 into[row] = own[at] + (line_in(part, 0, chunk)[row] + line_in(part, 1, chunk)[row])
 
             over_rows(eighth, 24, add)
+        sent(0, part, chunk)
+        launch(copies3[chunk][part])
+
+    def relay_blocks(part, chunk):
+        relay_sums(copies3[chunk][part], lambda distance, way: third_block(part, distance, way, chunk),
+                   lambda way: plane_relay(part, way, chunk))
+
+    def sum_blocks(part, chunk):
+        arrive(2, part, chunk, weight_out.at[2 * PARTS + part, pl.ds(0, 2 * block_rows), pl.ds(0, LANES)])
+        axis_b, axis_c = axes_of(part)[1:]
+        layer = layer_of(part, 0)
 
         def slot(index, which):
-            return plane(part, index, chunk).at[pl.ds(which * eighth, eighth)]
-
-        copies3[chunk].append(gather(2, part, chunk, axis_c, slot))
-        launch(copies3[chunk][part])
-
-    def sum_plane(part, chunk):
-        arrive(2, part, chunk, weight_out.at[2 * PARTS + part, pl.ds(0, 2 * quarter), columns(chunk)])
-        axis_b = axes_of(part)[1]
+            return mom_out.at[layer, *block_at(index, which, coord[axis_b] * quarter, chunk)]
+
+        for which in range(2):
+            into, own = slot(coord[axis_c], which), third_block(part, 0, which, chunk)
+            first, second = plane_in(part, 0, which, chunk), plane_in(part, 1, which, chunk)
+
+            def add(at, into=into, own=own, first=first, second=second):
+                into[at] = (own[at] + (first[at] + second[at])) * (1.0 / data_size)
+
+            over_rows(own.shape[0], 8, add)
+        sent(1, part, chunk)
+        copies4[chunk, part] = gather(3, part, chunk, axis_c, slot)
+        launch(copies4[chunk, part])
+
+    def gather_rows(part, chunk):
+        arrive(3, part, chunk, weight_out.at[0, pl.ds(0, 2 * block_rows), pl.ds(0, LANES)])
         layer = layer_of(part, 0)
-        one, two, three, four = (plane(part, slot, chunk) for slot in range(SIDE))
-
-        def add(at):
-            own_at = pl.ds(pl.multiple_of(coord[axis_b] * quarter + at.start, 8), at.size)
-            total = (one[at] + two[at]) + (three[at] + four[at])
-            mom_out[layer, own_at, columns(chunk)] = total * (1.0 / data_size)
-
-        over_rows(quarter, 48, add)
 
         def slot(index, which):
             return mom_out.at[layer, pl.ds(pl.multiple_of(index * quarter + which * eighth, 8), eighth), columns(chunk)]
 
-        copies4[chunk].append(gather(3, part, chunk, axis_b, slot))
-        launch(copies4[chunk][part])
-
-    def spread_mean(part, chunk):
-        arrive(3, part, chunk, mom_out.at[layer_of(part, 0), pl.ds(0, 2 * quarter), columns(chunk)])
+        sent(2, part, chunk)
+        copies5[chunk, part] = gather(4, part, chunk, axes_of(part)[1], slot)
+        launch(copies5[chunk, part])
+
+    def gather_means(part, chunk):
+        arrive(4, part, chunk, weight_out.at[0, pl.ds(0, 2 * quarter), columns(chunk)])
+        ends = [sum(GROUPS[:group + 1]) - 1 for group in range(len(GROUPS))]
+        if chunk not in ends:
+            return
+        group = ends.index(chunk)
 
         def slot(index, which):
-            return mom_out.at[part * SIDE + index, pl.ds(which * half, half), columns(chunk)]
-
-        copies5[chunk].append(gather(4, part, chunk, part, slot))
-        for copy in copies5[chunk][part][:2]:
+            return mom_out.at[part * SIDE + index, pl.ds(which * half, half), group_columns(group)]
+
+        sent(3, part, group)
+        copies6[group, part] = gather(5, part, group, part, slot)
+        for copy in copies6[group, part][:2]:
             copy.start()
 
     for part in parts:
         launch(copies1[0][part])
-    for part in parts:
-        for copy in copies1[1][part][:2]:
-            copy.start()
-    for part in parts:
-        forward(copies1[0][part])
-        for copy in copies1[1][part][2:4]:
-            copy.start()
-    for part in parts:
-        forward(copies1[1][part])
+
+    def ahead(chunk, kinds):
+        if chunk < CHUNKS:
+            for part in parts:
+                for kind in kinds:
+                    copies1[chunk][part][kind].start()
+
+    def forward_raw(part, chunk):
+        if part == 0 and chunk == 0:
+            ahead(1, (0, 1))
+        forward(copies1[chunk][part])
+        if part == PARTS - 1:
+            ahead(chunk + 1, (2, 3))
+            ahead(chunk + 2, (0, 1))
+
     for part in parts:
         fetch_raw[part].wait()
-        sum_raw(part, 0)
+    stages = [
+        forward_raw,
+        sum_raw,
+        relay_rows,
+        sum_rows,
+        relay_blocks,
+        sum_blocks,
+        lambda part, chunk: forward(copies4[chunk, part]),
+        gather_rows,
+        lambda part, chunk: forward(copies5[chunk, part]),
+        gather_means,
+    ]
+    for tick in range(len(stages) + CHUNKS - 1):
+        for chunk in reversed(chunks):
+            if 0 <= tick - chunk < len(stages):
+                for part in parts:
+                    stages[tick - chunk](part, chunk)
+    groups = range(len(GROUPS))
+    for group in groups:
+        for part in parts:
+            for copy in copies6[group, part][2:4]:
+                copy.start()
     for part in parts:
-        sum_raw(part, 1)
-    for chunk in chunks:
-        for part in parts:
-            sum_relay(part, chunk)
-    for chunk in chunks:
-        for part in parts:
-            sent(copies1[chunk][part])
-    for chunk in chunks:
-        for part in parts:
-            sum_line_in(part, chunk)
-    for chunk in chunks:
-        for part in parts:
-            forward(copies3[chunk][part])
-    for chunk in chunks:
-        for part in parts:
-            sent(copies2[chunk][part])
-    for chunk in chunks:
-        for part in parts:
-            sum_plane(part, chunk)
-    for chunk in chunks:
-        for part in parts:
-            forward(copies4[chunk][part])
-    for chunk in chunks:
-        for part in parts:
-            sent(copies3[chunk][part])
-    for chunk in chunks:
-        for part in parts:
-            spread_mean(part, chunk)
-    for chunk in chunks:
-        for part in parts:
-            for copy in copies5[chunk][part][2:4]:
-                copy.start()
-
-    swap_send, swap_receive = 2 * CHUNKS * PARTS * KINDS, (JOINED * 3 + KINDS) * CHUNKS * PARTS + KINDS * PARTS
+        for group in range(len(GROUPS), CHUNKS):
+            sent(3, part, group)
+
+    swap_send, swap_receive = 2 * CHUNKS * PARTS, JOINED * 3 * CHUNKS * PARTS + (len(GROUPS) + 1) * PARTS * KINDS
     for part in range(PARTS):
         fetch_mom[part].wait()
 
@@ -395,21 +458,21 @@
         def slot(index, which):
             return ortho_all.at[part * SIDE + index, pl.ds(which * half, half)]
 
-        copies6[0].append(gather(5, part, 0, part, slot))
-        launch(copies6[0][part])
+        copies7[part] = gather(6, part, 0, part, slot)
+        launch(copies7[part])
 
     give_first.wait_recv()
     orthogonalise(tp_idx, 0)
     swap_x = remote(x_buf.at[final, :, pl.ds(cols, cols)], ortho_all.at[first_layer], swap_send + 2, swap_receive + 2, partner)
     swap_x.start()
-    for chunk in chunks:
+    for group in groups:
         for part in parts:
-            forward(copies5[chunk][part])
+            forward(copies6[group, part])
     keep_half(first_layer)
     swap_x.wait()
     for chunk in chunks:
         for part in parts:
-            sent(copies4[chunk][part])
+            sent(4, part, chunk)
     ortho_gather(0)
     ortho_gather(1)
 
@@ -440,19 +503,16 @@
     fetch_turn[0].start()
     fetch_turn[1].start()
     for index, (part, distance) in enumerate(turns):
-        for chunk in chunks:
-            copies = copies5[chunk][part]
+        for group in groups:
             if distance == 0:
-                sent(copies[:4])
+                sent(5, part, group)
             elif distance == 3:
-                copies[2].wait_recv()
-                copies[4].wait_send()
+                copies6[group, part][2].wait_recv()
             elif distance == 1:
-                copies[3].wait_recv()
-                copies[5].wait_send()
+                copies6[group, part][3].wait_recv()
             else:
-                copies[4].wait_recv()
-                copies[5].wait_recv()
+                copies6[group, part][4].wait_recv()
+                copies6[group, part][5].wait_recv()
         fetch_turn[index].wait()
         layer = layer_of(part, distance)
 
@@ -464,19 +524,19 @@
             fetch_turn[index + 2].start()
 
     for part in range(PARTS):
-        forward(copies6[0][part])
+        forward(copies7[part])
     local(weight_ref, weight_out, weight_base).wait()
     for part, distance in turns:
         if distance == 3:
-            copies6[0][part][2].wait_recv()
+            copies7[part][2].wait_recv()
         elif distance == 1:
-            copies6[0][part][3].wait_recv()
+            copies7[part][3].wait_recv()
         elif distance == 2:
-            copies6[0][part][4].wait_recv()
-            copies6[0][part][5].wait_recv()
+            copies7[part][4].wait_recv()
+            copies7[part][5].wait_recv()
         descend(weight_out, ortho_all, rms_scale, layer_of(part, distance))
     for part in parts:
-        sent(copies6[0][part])
+        sent(6, part)
 
 
 def flush(held, mom_ref, weight_ref, sem):
@@ -498,8 +558,8 @@
 
     def per_device(weight, momentum, grad):
         layers, rows, cols = weight.shape
-        sends = 2 * CHUNKS * PARTS * KINDS + SWAPS
-        receives = (JOINED * 3 + KINDS) * CHUNKS * PARTS + KINDS * PARTS + SWAPS
+        sends = 2 * CHUNKS * PARTS + SWAPS
+        receives = JOINED * 3 * CHUNKS * PARTS + (len(GROUPS) + 1) * PARTS * KINDS + SWAPS
         rms_scale = 0.2 * math.sqrt(max(rows, cols * tp_size))
         bf16, f32 = jnp.bfloat16, jnp.float32
         in_hbm = pl.BlockSpec(memory_space=pltpu.HBM)

time: 193 us -> 191 us (0.990)
  Pallas kernels: 192 us -> 190 us
where the time goes in v6:
time: 191 us
  Pallas kernels  190 us (99%)
    pallas_call x1, Pallas kernels, per_device(): pl.pallas_call(functools.partial(kernel, rows, cols, data_size, rms_scale...  177 us
    pallas_call x1, Pallas kernels, per_device(): pl.pallas_call(flush, out_shape=(jax.ShapeDtypeStruct((layers, rows, cols...  13.6 us

profile of v6, /device:TPU:1, one launch (start us, length us, event | category | flops | bytes accessed | tf_op | source)
XLA Modules:
  0.0 190.8 jit_solution(11281812611824725638)
XLA Ops:
  0.6 176.6 %shard_map.50.held = f32[24,576,768]{2,1,0:T(8,128)S(1)} custom-call(bf16[12,576,768]{2,1,0:T(8,128)(2,1)} %bitcast.1, f32[12,576,768]{2,1,0:T(8,128)} %mom_ref.1, f32[12,576,768]{2,1,0:T(8,128)} %weight_ref.1), custom_call_target="tpu_custom_call" | custom-call | tf_op jit(solution)/shard_map/pallas_call | solution.py:567
  177.2 13.6 %shard_map.51 = (f32[12,576,768]{2,1,0:T(8,128)}, f32[12,576,768]{2,1,0:T(8,128)}) custom-call(f32[24,576,768]{2,1,0:T(8,128)S(1)} %shard_map.50.held), custom_call_target="tpu_custom_call" | custom-call | tf_op jit(solution)/shard_map/pallas_call | solution.py:584

commit v7 on v6

--- a/solution.py
+++ b/solution.py
@@ -21,6 +21,7 @@
 PARTS = 3
 STRIDES = (1, 4, 16)
 JOINED = 5
+LAST_KINDS = 4
 KINDS = 6
 CHUNKS = 3
 GROUPS = (2, 1)
@@ -143,25 +144,36 @@
     def numbers(phase, part, chunk, kind):
         group = chunk * PARTS + part
         send = phase % 2 * CHUNKS * PARTS + group
+        later = JOINED * CHUNKS * PARTS * 2
         if phase < JOINED:
-            return send, (phase * CHUNKS * PARTS + group) * 3 + min(kind, 2)
-        later = JOINED * 3 * CHUNKS * PARTS + (phase - JOINED) * len(GROUPS) * PARTS * KINDS
-        return send, later + group * KINDS + kind
-
-    def arrive(phase, part, chunk, landed):
-        remote(landed, landed, *numbers(phase, part, chunk, 2), partner).wait_recv()
+            return send, (phase * CHUNKS * PARTS + group) * 2 + (kind > 1)
+        if phase == JOINED:
+            return send, later + group * 2 + (kind > 1)
+        return send, later + len(GROUPS) * PARTS * 2 + part * LAST_KINDS + (0, 0, 1, 2, 3, 3)[kind]
+
+    def blocks(phase, chunk, count):
+        if phase == 0:
+            return ortho_all.at[pl.ds(0, count), :, columns(chunk)]
+        if phase in (1, 4):
+            return weight_out.at[0, pl.ds(0, count * quarter), columns(chunk)]
+        if phase in (2, 3):
+            return weight_out.at[0, pl.ds(0, count * block_rows), pl.ds(0, LANES)]
+        if phase == 5:
+            return mom_out.at[pl.ds(0, count), :, group_columns(chunk)]
+        return ortho_all.at[pl.ds(0, count)]
+
+    def await_blocks(phase, part, chunk, kind, count):
+        landed = blocks(phase, chunk, count)
+        remote(landed, landed, *numbers(phase, part, chunk, kind), partner).wait_recv()
+
+    def relayed(phase, part, chunk=0):
+        await_blocks(phase, part, chunk, 0, 1)
+
+    def arrive(phase, part, chunk=0):
+        await_blocks(phase, part, chunk, 2, 3 if phase == 0 else 2)
 
     def sent(phase, part, chunk=0):
-        if phase == 0:
-            left = ortho_all.at[pl.ds(0, SIDE), :, columns(chunk)]
-        elif phase in (1, 4):
-            left = weight_out.at[0, pl.ds(0, 3 * quarter), columns(chunk)]
-        elif phase in (2, 3):
-            left = weight_out.at[0, pl.ds(0, 3 * block_rows), pl.ds(0, LANES)]
-        elif phase == 5:
-            left = mom_out.at[pl.ds(0, 3), :, group_columns(chunk)]
-        else:
-            left = ortho_all.at[pl.ds(0, 3)]
+        left = blocks(phase, chunk, 4 if phase == 0 else 3)
         remote(left, left, *numbers(phase, part, chunk, 2), partner).wait_send()
 
     def group_columns(group):
@@ -206,7 +218,6 @@
 
     def relay_sums(copies, block, relay):
         for way, distance in ((0, 1), (1, 3)):
-            copies[way].wait_recv()
             into, own = relay(way), block(distance, way)
 
             def add(at, into=into, own=own):
@@ -246,10 +257,9 @@
         for copy in copies[:4]:
             copy.start()
 
-    def forward(copies):
-        copies[0].wait_recv()
+    def forward(copies, *where):
+        relayed(*where)
         copies[4].start()
-        copies[1].wait_recv()
         copies[5].start()
 
     fetch_raw, fetch_mom = [], []
@@ -271,7 +281,7 @@
     copies4, copies5, copies6, copies7 = ({}, {}, {}, {})
 
     def sum_raw(part, chunk):
-        arrive(0, part, chunk, ortho_all.at[pl.ds(part * 3, 3), :, columns(chunk)])
+        arrive(0, part, chunk)
         own, into = raw_own(part, chunk), sum_line(part, chunk)
         first, second, third = (raw_in(part, slot, chunk) for slot in range(3))
 
@@ -283,11 +293,12 @@
         launch(copies2[chunk][part])
 
     def relay_rows(part, chunk):
+        relayed(1, part, chunk)
         relay_sums(copies2[chunk][part], lambda distance, way: line_block(part, distance, way, chunk),
                    lambda way: line_relay(part, way, chunk))
 
     def sum_rows(part, chunk):
-        arrive(1, part, chunk, weight_out.at[PARTS + part, pl.ds(0, 2 * quarter), columns(chunk)])
+        arrive(1, part, chunk)
         into = plane(part, chunk)
         for which in range(2):
             own = line_block(part, 0, which, chunk)
@@ -301,11 +312,12 @@
         launch(copies3[chunk][part])
 
     def relay_blocks(part, chunk):
+        relayed(2, part, chunk)
         relay_sums(copies3[chunk][part], lambda distance, way: third_block(part, distance, way, chunk),
                    lambda way: plane_relay(part, way, chunk))
 
     def sum_blocks(part, chunk):
-        arrive(2, part, chunk, weight_out.at[2 * PARTS + part, pl.ds(0, 2 * block_rows), pl.ds(0, LANES)])
+        arrive(2, part, chunk)
         axis_b, axis_c = axes_of(part)[1:]
         layer = layer_of(part, 0)
 
@@ -325,7 +337,7 @@
         launch(copies4[chunk, part])
 
     def gather_rows(part, chunk):
-        arrive(3, part, chunk, weight_out.at[0, pl.ds(0, 2 * block_rows), pl.ds(0, LANES)])
+        arrive(3, part, chunk)
         layer = layer_of(part, 0)
 
         def slot(index, which):
@@ -336,7 +348,7 @@
         launch(copies5[chunk, part])
 
     def gather_means(part, chunk):
-        arrive(4, part, chunk, weight_out.at[0, pl.ds(0, 2 * quarter), columns(chunk)])
+        arrive(4, part, chunk)
         ends = [sum(GROUPS[:group + 1]) - 1 for group in range(len(GROUPS))]
         if chunk not in ends:
             return
@@ -362,7 +374,7 @@
     def forward_raw(part, chunk):
         if part == 0 and chunk == 0:
             ahead(1, (0, 1))
-        forward(copies1[chunk][part])
+        forward(copies1[chunk][part], 0, part, chunk)
         if part == PARTS - 1:
             ahead(chunk + 1, (2, 3))
             ahead(chunk + 2, (0, 1))
@@ -376,9 +388,9 @@
         sum_rows,
         relay_blocks,
         sum_blocks,
-        lambda part, chunk: forward(copies4[chunk, part]),
+        lambda part, chunk: forward(copies4[chunk, part], 3, part, chunk),
         gather_rows,
-        lambda part, chunk: forward(copies5[chunk, part]),
+        lambda part, chunk: forward(copies5[chunk, part], 4, part, chunk),
         gather_means,
     ]
     for tick in range(len(stages) + CHUNKS - 1):
@@ -395,7 +407,7 @@
         for group in range(len(GROUPS), CHUNKS):
             sent(3, part, group)
 
-    swap_send, swap_receive = 2 * CHUNKS * PARTS, JOINED * 3 * CHUNKS * PARTS + (len(GROUPS) + 1) * PARTS * KINDS
+    swap_send, swap_receive = 2 * CHUNKS * PARTS, JOINED * CHUNKS * PARTS * 2 + PARTS * (len(GROUPS) * 2 + LAST_KINDS)
     for part in range(PARTS):
         fetch_mom[part].wait()
 
@@ -417,7 +429,7 @@
     for fetch in fetch_weight[PARTS:]:
         fetch.start()
 
-    def orthogonalise(part, which):
+    def orthogonalise(part, which, ready=None):
         def squares(index, total):
             at = pl.ds(pl.multiple_of(index * 8, 8), 8)
             own, other = weight_out[part, at], nest_in[which, at]
@@ -431,6 +443,8 @@
             x_buf[0, at, pl.ds(cols, cols)] = (nest_in[which, at] * scale).astype(jnp.bfloat16)
 
         over_rows(rows, 16, normalise)
+        if ready is not None:
+            ready()
 
         def newton(step, carry):
             now = lax.rem(step, 2)
@@ -454,12 +468,11 @@
             ortho_all[layer, at] = x_buf[final, at, pl.ds(0, cols)]
         over_rows(rows, 16, move)
 
-    def ortho_gather(part):
-        def slot(index, which):
+    for part in parts:
+        def slot(index, which, part=part):
             return ortho_all.at[part * SIDE + index, pl.ds(which * half, half)]
 
         copies7[part] = gather(6, part, 0, part, slot)
-        launch(copies7[part])
 
     give_first.wait_recv()
     orthogonalise(tp_idx, 0)
@@ -467,31 +480,34 @@
     swap_x.start()
     for group in groups:
         for part in parts:
-            forward(copies6[group, part])
+            forward(copies6[group, part], 5, part, group)
     keep_half(first_layer)
-    swap_x.wait()
     for chunk in chunks:
         for part in parts:
             sent(4, part, chunk)
-    ortho_gather(0)
-    ortho_gather(1)
-
     give_x = remote(x_buf.at[final, :, pl.ds(cols, cols)], ortho_all.at[layer_of(2, 0)], swap_send + 3, swap_receive + 3, partner)
 
     @pl.when(tp_idx == 0)
     def _():
+        launch(copies7[0])
         give_second.wait_recv()
-        orthogonalise(2, 1)
+        orthogonalise(2, 1, swap_x.wait_send)
         give_x.start()
         keep_half(layer_of(2, 0))
+        launch(copies7[2])
+        swap_x.wait_recv()
+        launch(copies7[1])
         give_x.wait_send()
 
     @pl.when(tp_idx == 1)
     def _():
+        launch(copies7[1])
+        swap_x.wait()
+        launch(copies7[0])
         give_x.wait_recv()
+        launch(copies7[2])
         give_second.wait_send()
 
-    ortho_gather(2)
     give_first.wait_send()
     for fetch in fetch_weight[:PARTS]:
         fetch.start()
@@ -507,12 +523,7 @@
             if distance == 0:
                 sent(5, part, group)
             elif distance == 3:
-                copies6[group, part][2].wait_recv()
-            elif distance == 1:
-                copies6[group, part][3].wait_recv()
-            else:
-                copies6[group, part][4].wait_recv()
-                copies6[group, part][5].wait_recv()
+                arrive(5, part, group)
         fetch_turn[index].wait()
         layer = layer_of(part, distance)
 
@@ -524,7 +535,7 @@
             fetch_turn[index + 2].start()
 
     for part in range(PARTS):
-        forward(copies7[part])
+        forward(copies7[part], 6, part)
     local(weight_ref, weight_out, weight_base).wait()
     for part, distance in turns:
         if distance == 3:
@@ -532,8 +543,7 @@
         elif distance == 1:
             copies7[part][3].wait_recv()
         elif distance == 2:
-            copies7[part][4].wait_recv()
-            copies7[part][5].wait_recv()
+            await_blocks(6, part, 0, 4, 1)
         descend(weight_out, ortho_all, rms_scale, layer_of(part, distance))
     for part in parts:
         sent(6, part)
@@ -559,7 +569,7 @@
     def per_device(weight, momentum, grad):
         layers, rows, cols = weight.shape
         sends = 2 * CHUNKS * PARTS + SWAPS
-        receives = JOINED * 3 * CHUNKS * PARTS + (len(GROUPS) + 1) * PARTS * KINDS + SWAPS
+        receives = JOINED * CHUNKS * PARTS * 2 + PARTS * (len(GROUPS) * 2 + LAST_KINDS) + SWAPS
         rms_scale = 0.2 * math.sqrt(max(rows, cols * tp_size))
         bf16, f32 = jnp.bfloat16, jnp.float32
         in_hbm = pl.BlockSpec(memory_space=pltpu.HBM)

time: 191 us -> 189 us (0.990); the launches traced: 191 us -> 186 us
  Pallas kernels: 190 us -> 185 us
    pallas_call x1, Pallas kernels: 177 us -> 172 us  [per_device(): pl.pallas_call(functools.partial(kernel, rows, cols, data_size, rms_scale...]
where the time goes in v7:
time: 189 us; the launch traced here: 186 us
  Pallas kernels  185 us (98%)
    pallas_call x1, Pallas kernels, per_device(): pl.pallas_call(functools.partial(kernel, rows, cols, data_size, rms_scale...  172 us
    pallas_call x1, Pallas kernels, per_device(): pl.pallas_call(flush, out_shape=(jax.ShapeDtypeStruct((layers, rows, cols...  13.6 us

profile of v7, /device:TPU:1, one launch (start us, length us, event | category | flops | bytes accessed | tf_op | source)
XLA Modules:
  0.0 186.1 jit_solution(13274301324753568070)
XLA Ops:
  0.6 171.8 %shard_map.50.held = f32[24,576,768]{2,1,0:T(8,128)S(1)} custom-call(bf16[12,576,768]{2,1,0:T(8,128)(2,1)} %bitcast.1, f32[12,576,768]{2,1,0:T(8,128)} %mom_ref.1, f32[12,576,768]{2,1,0:T(8,128)} %weight_ref.1), custom_call_target="tpu_custom_call" | custom-call | tf_op jit(solution)/shard_map/pallas_call | solution.py:577
  172.5 13.6 %shard_map.51 = (f32[12,576,768]{2,1,0:T(8,128)}, f32[12,576,768]{2,1,0:T(8,128)}) custom-call(f32[24,576,768]{2,1,0:T(8,128)S(1)} %shard_map.50.held), custom_call_target="tpu_custom_call" | custom-call | tf_op jit(solution)/shard_map/pallas_call | solution.py:594

commit v8 on v7

--- a/solution.py
+++ b/solution.py
@@ -24,6 +24,7 @@
 LAST_KINDS = 4
 KINDS = 6
 CHUNKS = 3
+WHOLE = 1
 GROUPS = (2, 1)
 LANES = 128
 SPLIT = 40
@@ -100,8 +101,9 @@
         lane = chunk * width + lax.rem(index, 2) * LANES
         return pl.ds(pl.multiple_of(at, 8), size), pl.ds(pl.multiple_of(lane, LANES), LANES)
 
-    def plane(part, chunk):
-        return weight_out.at[2 * PARTS + part, pl.ds(0, quarter), columns(chunk)]
+    def plane(part, chunk, slot=0):
+        at = pl.ds(pl.multiple_of(slot * quarter, 8), quarter)
+        return weight_out.at[2 * PARTS + part, at, columns(chunk)]
 
     def plane_block(part, index, which, chunk):
         return weight_out.at[2 * PARTS + part, *block_at(index, which, 0, chunk)]
@@ -154,7 +156,7 @@
     def blocks(phase, chunk, count):
         if phase == 0:
             return ortho_all.at[pl.ds(0, count), :, columns(chunk)]
-        if phase in (1, 4):
+        if phase in (1, 4) or (phase == 2 and chunk < WHOLE):
             return weight_out.at[0, pl.ds(0, count * quarter), columns(chunk)]
         if phase in (2, 3):
             return weight_out.at[0, pl.ds(0, count * block_rows), pl.ds(0, LANES)]
@@ -277,7 +279,14 @@
     chunks, parts = range(CHUNKS), range(PARTS)
     copies1 = [[spread(part, chunk) for part in parts] for chunk in chunks]
     copies2 = [[reduce_rows(part, chunk) for part in parts] for chunk in chunks]
-    copies3 = [[reduce_blocks(part, chunk) for part in parts] for chunk in chunks]
+
+    def exchange(part, chunk):
+        def slot(index, which):
+            return plane(part, chunk, index).at[pl.ds(which * eighth, eighth)]
+
+        return gather(2, part, chunk, axes_of(part)[2], slot)
+
+    copies3 = [[(exchange if chunk < WHOLE else reduce_blocks)(part, chunk) for part in parts] for chunk in chunks]
     copies4, copies5, copies6, copies7 = ({}, {}, {}, {})
 
     def sum_raw(part, chunk):
@@ -299,7 +308,7 @@
 
     def sum_rows(part, chunk):
         arrive(1, part, chunk)
-        into = plane(part, chunk)
+        into = plane(part, chunk, coord[axes_of(part)[2]] if chunk < WHOLE else 0)
         for which in range(2):
             own = line_block(part, 0, which, chunk)
 
@@ -336,8 +345,24 @@
         copies4[chunk, part] = gather(3, part, chunk, axis_c, slot)
         launch(copies4[chunk, part])
 
+    def sum_planes(part, chunk):
+        arrive(2, part, chunk)
+        layer, axis_b = layer_of(part, 0), axes_of(part)[1]
+        one, two, three, four = (plane(part, chunk, slot) for slot in range(SIDE))
+        into = mom_out.at[layer, pl.ds(pl.multiple_of(coord[axis_b] * quarter, 8), quarter), columns(chunk)]
+
+        def add(at):
+            into[at] = ((one[at] + two[at]) + (three[at] + four[at])) * (1.0 / data_size)
+
+        over_rows(quarter, 48, add)
+        sent(1, part, chunk)
+        spread_rows(part, chunk)
+
     def gather_rows(part, chunk):
         arrive(3, part, chunk)
+        spread_rows(part, chunk)
+
+    def spread_rows(part, chunk):
         layer = layer_of(part, 0)
 
         def slot(index, which):
@@ -357,7 +382,8 @@
         def slot(index, which):
             return mom_out.at[part * SIDE + index, pl.ds(which * half, half), group_columns(group)]
 
-        sent(3, part, group)
+        if group >= WHOLE:
+            sent(3, part, group)
         copies6[group, part] = gather(5, part, group, part, slot)
         for copy in copies6[group, part][:2]:
             copy.start()
@@ -393,11 +419,20 @@
         lambda part, chunk: forward(copies5[chunk, part], 4, part, chunk),
         gather_means,
     ]
+    stages_whole = stages[:4] + [
+        lambda part, chunk: forward(copies3[chunk][part], 2, part, chunk),
+        sum_planes,
+        None,
+        stages[8],
+        None,
+        gather_means,
+    ]
     for tick in range(len(stages) + CHUNKS - 1):
         for chunk in reversed(chunks):
             if 0 <= tick - chunk < len(stages):
-                for part in parts:
-                    stages[tick - chunk](part, chunk)
+                stage = (stages_whole if chunk < WHOLE else stages)[tick - chunk]
+                for part in parts if stage else ():
+                    stage(part, chunk)
     groups = range(len(GROUPS))
     for group in groups:
         for part in parts:

time: 189 us -> 190 us (level)
  no operation moved by 1% of the time
where the time goes in v8:
time: 190 us; the launch traced here: 187 us
  Pallas kernels  186 us (98%)
    pallas_call x1, Pallas kernels, per_device(): pl.pallas_call(functools.partial(kernel, rows, cols, data_size, rms_scale...  173 us
    pallas_call x1, Pallas kernels, per_device(): pl.pallas_call(flush, out_shape=(jax.ShapeDtypeStruct((layers, rows, cols...  13.6 us

profile of v8, /device:TPU:1, one launch (start us, length us, event | category | flops | bytes accessed | tf_op | source)
XLA Modules:
  0.0 187.0 jit_solution(2703678299445360411)
XLA Ops:
  0.6 172.7 %shard_map.50.held = f32[24,576,768]{2,1,0:T(8,128)S(1)} custom-call(bf16[12,576,768]{2,1,0:T(8,128)(2,1)} %bitcast.1, f32[12,576,768]{2,1,0:T(8,128)} %mom_ref.1, f32[12,576,768]{2,1,0:T(8,128)} %weight_ref.1), custom_call_target="tpu_custom_call" | custom-call | tf_op jit(solution)/shard_map/pallas_call | solution.py:612
  173.4 13.6 %shard_map.51 = (f32[12,576,768]{2,1,0:T(8,128)}, f32[12,576,768]{2,1,0:T(8,128)}) custom-call(f32[24,576,768]{2,1,0:T(8,128)S(1)} %shard_map.50.held), custom_call_target="tpu_custom_call" | custom-call | tf_op jit(solution)/shard_map/pallas_call | solution.py:629

commit v9 on v7

--- a/solution.py
+++ b/solution.py
@@ -24,7 +24,7 @@
 LAST_KINDS = 4
 KINDS = 6
 CHUNKS = 3
-GROUPS = (2, 1)
+GROUPS = (1, 1, 1)
 LANES = 128
 SPLIT = 40
 SWAPS = 4

time: 189 us -> 192 us (1.016); the launches traced: 186 us -> 191 us
  Pallas kernels: 185 us -> 191 us
    pallas_call x1, Pallas kernels: 172 us -> 177 us  [per_device(): pl.pallas_call(functools.partial(kernel, rows, cols, data_size, rms_scale...]
where the time goes in v9:
time: 192 us; the launch traced here: 191 us
  Pallas kernels  191 us (99%)
    pallas_call x1, Pallas kernels, per_device(): pl.pallas_call(functools.partial(kernel, rows, cols, data_size, rms_scale...  177 us
    pallas_call x1, Pallas kernels, per_device(): pl.pallas_call(flush, out_shape=(jax.ShapeDtypeStruct((layers, rows, cols...  13.6 us

profile of v9, /device:TPU:1, one launch (start us, length us, event | category | flops | bytes accessed | tf_op | source)
XLA Modules:
  0.0 191.4 jit_solution(13752565602701546980)
XLA Ops:
  0.6 177.2 %shard_map.50.held = f32[24,576,768]{2,1,0:T(8,128)S(1)} custom-call(bf16[12,576,768]{2,1,0:T(8,128)(2,1)} %bitcast.1, f32[12,576,768]{2,1,0:T(8,128)} %mom_ref.1, f32[12,576,768]{2,1,0:T(8,128)} %weight_ref.1), custom_call_target="tpu_custom_call" | custom-call | tf_op jit(solution)/shard_map/pallas_call | solution.py:577
  177.8 13.6 %shard_map.51 = (f32[12,576,768]{2,1,0:T(8,128)}, f32[12,576,768]{2,1,0:T(8,128)}) custom-call(f32[24,576,768]{2,1,0:T(8,128)S(1)} %shard_map.50.held), custom_call_target="tpu_custom_call" | custom-call | tf_op jit(solution)/shard_map/pallas_call | solution.py:594
